TPU v7x, 256 devices: a whole 4x4x8 slice. The times are simulated.
256 devices in a mesh: grp: 32 (over x, z), node: 8 (over y, core).
Axes of the slice: x: 4, y: 4, z: 8, core: 2. Of those that a mesh axis runs over, the one named last changes fastest.
Arguments:
- initial: float32 [6, 32, 262144], P(None, None, ('grp', 'node')), may hold values from -0.5 to 16, as said below
- afferent_noise_level: float32 [32, 262144], P(None, ('grp', 'node')), may hold values from 0.12 to 0.32
- history: bfloat16 [64, 32, 262144], P(None, None, ('grp', 'node')), may hold values from 0 to 1
- weights: bfloat16 [256, 24, 128, 1024], P(('grp', 'node')), may hold values from -0.109375 to 0.109375
- lead_field: bfloat16 [128, 262144], P(None, ('grp', 'node')), may hold values from -0.0014648438 to 0.0014648438
- src_group: int32 [256, 24], replicated, may hold values from 0 to 31, as said below
- src_sub: int32 [256, 24], replicated, may hold values from 0 to 7
- delays: int32 [256, 24], replicated, may hold values from 6 to 63
- counts: int32 [256], replicated, may hold values from 16 to 24, as said below
Outputs:
- final_state: float32 [6, 32, 262144], P(None, None, ('grp', 'node'))
- sensors: float32 [6, 128, 32], replicated
Inputs may be any that keep to these rules, and one draw needn't show every extreme that they name: `initial`: rows 0 to 2 are potentials and rows 3 to 5 their rates; row 0 lies within 0 and 0.4, row 1 within 4 and 16, row 2 within 0 and 8, rows 3 to 5 within -0.5 and 0.5. `src_group`: among the tiles k < counts[b] of a block b no owner group appears more than 1 times, and some block reaches 1. Tiles k >= counts[b] of block b are ignored; in every draw some block has 24 live tiles.
All inputs are finite; a program needn't handle non-finite values.
Results may differ from a plain program's by a relative error of at most 0.0003.
The roundings to bfloat16 on the way count: a program that leaves them out, or rounds other values in their place, can miss the bound.
Values may be sent and summed in bfloat16 or wider, within the bound.
No kernel may reach another device: no remote copies, remote signals or barrier semaphores. Data moves between devices by JAX's collectives and lax.ppermute only.
A program may use at most 128 MiB of HBM per device.

v0:
```python
import jax
import jax.numpy as jnp
from jax import lax
from jax.sharding import Mesh
from jax.sharding import PartitionSpec as P

DMIN = 6
STEPS = 6
GRP = ("grp_0", "grp_1")
NODE = ("node_0", "node_1")
GRP_NODE = ("grp_0", "grp_1", "node_0", "node_1")


exciting_amplitude = 3.25
suppressive_amplitude = 22.0
exciting_inverse_lag = 0.1
suppressive_inverse_lag = 0.05
link_factor = 135.0
maximal_spike_frequency = 0.005
thresh = 6.0
fire_slope = 0.56
global_scaling_factor = 0.5
dt_step = 0.5


def rows_for(lines, length):
    spare = -lines.shape[0] % length
    if not spare:
        return lines
    return jnp.concatenate([lines, jnp.zeros((spare, *lines.shape[1:]), lines.dtype)])


def from_everyone(x, axis):
    copies = jnp.broadcast_to(x, (lax.axis_size(axis), *x.shape))
    return lax.all_to_all(copies, axis, split_axis=0, concat_axis=0, tiled=True)


def laid_out(blocks, dim):
    blocks = jnp.moveaxis(blocks, 0, dim)
    lengths = blocks.shape
    return blocks.reshape(*lengths[:dim], lengths[dim] * lengths[dim + 1], *lengths[dim + 2 :])


def gather_axes(x, axes, dim):
    far, near = axes
    blocks = from_everyone(from_everyone(x, far), near)
    return laid_out(blocks.swapaxes(0, 1).reshape(-1, *x.shape), dim)


def split_up(x, dim, length):
    before, after = (x.shape[:dim], x.shape[dim + 1 :])
    return jnp.moveaxis(x.reshape(*before, length, -1, *after), dim, 0)


def sent_and_summed(x, axis, dim):
    length = lax.axis_size(axis)
    blocks = lax.all_to_all(split_up(x, dim, length), axis, 0, 0, tiled=True)
    return jnp.sum(blocks, axis=0)


def sum_in_two_steps(x, axes, dim):
    far, near = axes
    blocks = split_up(x, dim, lax.axis_size(far))
    nearer = sent_and_summed(blocks, near, dim + 1)
    arrived = lax.all_to_all(nearer, far, split_axis=0, concat_axis=0, tiled=True)
    return arrived.sum(axis=0)


def total_of(x, axes):
    lines = x.reshape(-1, x.shape[-1])
    padded = rows_for(lines, lax.axis_size(axes[0]) * lax.axis_size(axes[1]))
    whole = gather_axes(sum_in_two_steps(padded, axes, 0), axes, 0)
    return lax.slice_in_dim(whole, 0, len(lines)).reshape(x.shape)


def sigmoid_spike_density(somatic_charge_level):
    return 1.0 / (1.0 + jnp.exp(fire_slope * (thresh - somatic_charge_level)))


def derivative(population_variables, afferent_noise_level, network_afferent):
    principal_cell_level, interneuron_depolarization, suppressive_depolarization = (
        population_variables[0],
        population_variables[1],
        population_variables[2],
    )
    principal_cell_curvature = (
        exciting_amplitude
        * exciting_inverse_lag
        * maximal_spike_frequency
        * sigmoid_spike_density(interneuron_depolarization - suppressive_depolarization)
        - 2.0 * exciting_inverse_lag * population_variables[3]
        - exciting_inverse_lag * exciting_inverse_lag * principal_cell_level
    )
    interneuron_second_derivative = (
        exciting_amplitude
        * exciting_inverse_lag
        * (
            afferent_noise_level
            + 0.8
            * link_factor
            * maximal_spike_frequency
            * sigmoid_spike_density(link_factor * principal_cell_level)
            + global_scaling_factor * network_afferent
        )
        - 2.0 * exciting_inverse_lag * population_variables[4]
        - exciting_inverse_lag * exciting_inverse_lag * interneuron_depolarization
    )
    suppressive_second_derivative = (
        suppressive_amplitude
        * suppressive_inverse_lag
        * 0.25
        * link_factor
        * maximal_spike_frequency
        * sigmoid_spike_density(0.25 * link_factor * principal_cell_level)
        - 2.0 * suppressive_inverse_lag * population_variables[5]
        - suppressive_inverse_lag * suppressive_inverse_lag * suppressive_depolarization
    )
    return jnp.stack(
        [
            population_variables[3],
            population_variables[4],
            population_variables[5],
            principal_cell_curvature,
            interneuron_second_derivative,
            suppressive_second_derivative,
        ]
    )


def advance(population_variables, afferent_noise_level, coupled_now, coupled_next):
    first_rate = derivative(population_variables, afferent_noise_level, coupled_now)
    second_rate = derivative(
        population_variables + dt_step * first_rate, afferent_noise_level, coupled_next
    )
    return population_variables + 0.5 * dt_step * (first_rate + second_rate)


def body(
    initial, afferent_noise_level, history, weights, lead_field, src_group, src_sub, delays, counts
):
    owners = lax.axis_size(GRP)
    columns = lax.axis_size(NODE)
    my_group = lax.axis_index(GRP)
    my_column = lax.axis_index(NODE)
    myself = my_group * columns + my_column
    cycle_len, replicas, block_len = history.shape
    tiles_max = src_group.shape[1]
    piece_len = weights.shape[2]
    slots_per = (tiles_max + owners - 1) // owners
    zero_index = jnp.zeros((), jnp.int32)
    tile_lanes = jnp.arange(tiles_max, dtype=jnp.int32)
    places = jnp.arange(slots_per, dtype=jnp.int32)
    tile_stack = weights.reshape(tiles_max * piece_len, block_len)

    def column_of(lookup):
        return lax.dynamic_index_in_dim(lookup.reshape(owners, columns, -1), my_column, 1, False)

    col_group = column_of(src_group)
    col_sub = column_of(src_sub)
    col_delay = column_of(delays)
    col_count = column_of(counts)[:, 0]
    matched = (col_group == my_group) & (tile_lanes[None, :] < col_count[:, None])
    ranked = jnp.cumsum(matched.astype(jnp.int32), axis=1) - 1
    picked_slot = matched[:, :, None] & (ranked[:, :, None] == places[None, None, :])
    sel_sub = jnp.sum(jnp.where(picked_slot, col_sub[:, :, None], 0), axis=1)
    sel_delay = jnp.sum(jnp.where(picked_slot, col_delay[:, :, None], 0), axis=1)
    own_group = lax.dynamic_index_in_dim(src_group, myself, 0, False)
    own_count = lax.dynamic_index_in_dim(counts, myself, 0, False)
    own_live = tile_lanes < own_count
    earlier = (
        (own_group[:, None] == own_group[None, :])
        & own_live[None, :]
        & (tile_lanes[None, :] < tile_lanes[:, None])
    )
    own_rank = jnp.minimum(jnp.sum(earlier.astype(jnp.int32), axis=1), slots_per - 1)
    own_mask = own_live.astype(jnp.bfloat16)

    def pack(cycle, in_times):
        how_many = in_times.shape[0]
        slot_ids = jnp.mod(in_times[None, :, None] - sel_delay[:, None, :], cycle_len)
        starts = jnp.broadcast_to(sel_sub[:, None, :] * piece_len, slot_ids.shape)

        def cut_piece(slot_id, start_id):
            return lax.dynamic_slice(
                cycle, (slot_id, zero_index, start_id), (1, replicas, piece_len)
            )[0]

        pieces = jax.vmap(cut_piece)(slot_ids.reshape(-1), starts.reshape(-1))
        return pieces.reshape(owners, how_many, slots_per, replicas, piece_len)

    def unpack(parcel):
        how_many = parcel.shape[1]
        picked = parcel[own_group, :, own_rank] * own_mask[:, None, None, None]
        flattened = jnp.transpose(picked, (1, 2, 0, 3)).reshape(
            how_many * replicas, tiles_max * piece_len
        )
        return jnp.dot(flattened, tile_stack, preferred_element_type=jnp.float32).reshape(
            how_many, replicas, block_len
        )

    def store_fire(cycle, population_variables, step_id):
        spike_density_result = sigmoid_spike_density(
            population_variables[1] - population_variables[2]
        ).astype(jnp.bfloat16)
        return lax.dynamic_update_slice(
            cycle, spike_density_result[None], (jnp.mod(step_id, cycle_len), zero_index, zero_index)
        )

    def record(sensors, population_variables, step_id):
        potential = (population_variables[1] - population_variables[2]).astype(jnp.bfloat16)
        local_sum = lax.dot_general(
            lead_field, potential, (((1,), (1,)), ((), ())), preferred_element_type=jnp.float32
        )
        return lax.dynamic_update_slice(sensors, local_sum[None], (step_id, zero_index, zero_index))

    start_times = jnp.zeros((1,), jnp.int32)
    network_afferent = unpack(
        lax.all_to_all(pack(history, start_times), GRP, split_axis=0, concat_axis=0, tiled=True)
    )[0]
    sensors = jnp.zeros((STEPS, lead_field.shape[0], replicas), jnp.float32)

    def one_batch(batch_id, carried):
        population_variables, cycle, coupled_now, sensors = carried
        base_step = (jnp.asarray(batch_id) * DMIN).astype(jnp.int32)
        cycle = store_fire(cycle, population_variables, base_step)
        in_times = base_step + 1 + jnp.arange(DMIN, dtype=jnp.int32)
        batch_input = unpack(
            lax.all_to_all(pack(cycle, in_times), GRP, split_axis=0, concat_axis=0, tiled=True)
        )
        for offset in range(DMIN):
            step_id = base_step + offset
            if offset > 0:
                cycle = store_fire(cycle, population_variables, step_id)
            population_variables = advance(
                population_variables, afferent_noise_level, coupled_now, batch_input[offset]
            )
            coupled_now = batch_input[offset]
            sensors = record(sensors, population_variables, step_id)
        return (population_variables, cycle, coupled_now, sensors)

    population_variables, cycle, network_afferent, sensors = lax.fori_loop(
        0, STEPS // DMIN, one_batch, (initial, history, network_afferent, sensors)
    )
    sensors = total_of(sensors, (("grp_0", "grp_1"), ("node_0", "node_1")))
    return (population_variables, sensors)


def solution(mesh):
    finer = Mesh(mesh.devices.reshape(4, 8, 4, 2), ("grp_0", "grp_1", "node_0", "node_1"))
    placed = (
        P(None, None, GRP_NODE),
        P(None, GRP_NODE),
        P(None, None, GRP_NODE),
        P(GRP_NODE, None, None, None),
        P(None, GRP_NODE),
        P(),
        P(),
        P(),
        P(),
    )
    return jax.shard_map(
        body, mesh=finer, in_specs=placed, out_specs=(P(None, None, GRP_NODE), P()), check_vma=False
    )
```

profile of v0, /device:TPU:1, one launch (start us, length us, event | category | flops | bytes accessed | tf_op | source)
XLA Modules:
  0.0 220.9 jit_solution(7747169027593972095)
XLA Ops:
  0.7 0.8 reshape.599
  1.5 0.8 copy.89
  2.8 0.8 copy.91
  3.6 0.8 copy.92
  4.4 23.1 %copy.93 = bf16[64,32,1024]{1,0,2:T(8,128)(2,1)} copy(bf16[64,32,1024]{2,1,0:T(8,128)(2,1)} %param.11) | data formatting | bytes 8388608 | tf_op args[2]
  27.8 5.9 %gather_fusion = bf16[32,32,128]{1,0,2:T(8,128)(2,1)S(1)} fusion(bf16[64,32,1024]{1,0,2:T(8,128)(2,1)} %copy.93, s32[32]{0:T(128)S(1)} %fusion.192), kind=kCustom, calls=%fused_computation | custom fusion | bytes 524672 | tf_op jit(solution)/shard_map/vmap()/gather | solution.py:184
  33.7 1.8 copy.94
  35.5 11.8 %all-to-all-start = ((bf16[32,1,1,32,128]{4,3,2,1,0:T(8,128)(2,1)}), bf16[32,1,1,32,128]{4,3,2,1,0:T(8,128)(2,1)S(1)}, u32[]{:S(2)}, u32[]{:S(2)}) async-start(bf16[32,1,1,32,128]{4,3,2,1,0:T(8,128)(2,1)} %copy.94), calls=%async_computation | async-start | bytes 524288 | tf_op jit(solution)/shard_map/all_to_all | solution.py:218
  47.8 0.8 fusion.194
  48.9 14.6 %dynamic_update_slice.38 = bf16[64,32,1024]{1,0,2:T(8,128)(2,1)} dynamic-update-slice(bf16[64,32,1024]{1,0,2:T(8,128)(2,1)} %copy.93, bf16[1,32,1024]{1,0,2:T(2,128)(2,1)S(1)} %copy.96, s32[]{:T(128)} %constant.168.clone.1, s32[]{:T(128)} %constant.168.clone.1, s32[]{:T(128)} %constant.168.clone.1) | dynamic-update-slice | bytes 131076 | tf_op jit(solution)/shard_map/while/body/eval_jaxpr/dynamic_update_slice | solution.py:205
  63.5 33.1 %gather_fusion.2 = bf16[192,32,128]{1,0,2:T(8,128)(2,1)} fusion(bf16[64,32,1024]{1,0,2:T(8,128)(2,1)} %dynamic_update_slice.38, s32[192]{0:T(256)S(1)} %bitcast.389), kind=kCustom, calls=%fused_computation.2 | custom fusion | bytes 3148032 | tf_op jit(solution)/shard_map/while/body/eval_jaxpr/vmap()/gather | solution.py:184
  96.6 8.9 %copy.97 = bf16[192,32,128]{2,1,0:T(8,128)(2,1)} copy(bf16[192,32,128]{1,0,2:T(8,128)(2,1)} %gather_fusion.2) | data formatting | bytes 3145728 | tf_op jit(solution)/shard_map/while/body/eval_jaxpr/vmap()/gather | solution.py:184
  105.5 9.2 %all-to-all-start.1 = ((bf16[32,6,1,32,128]{4,3,1,2,0:T(8,128)(2,1)}), bf16[32,6,1,32,128]{4,3,1,2,0:T(8,128)(2,1)S(1)}, u32[]{:S(2)}, u32[]{:S(2)}) async-start(bf16[32,6,1,32,128]{4,3,1,2,0:T(8,128)(2,1)} %bitcast.28), calls=%async_computation.1 | async-start | bytes 3145728 | tf_op jit(solution)/shard_map/while/body/eval_jaxpr/all_to_all | solution.py:228
  114.7 0.8 slice.426
  116.3 0.7 iota_compare_fusion.3
  116.9 0.7 fusion.193
  117.8 0.6 gather_fusion.1
  118.5 4.1 %fusion.23 = f32[1,32,1024]{2,1,0:T(8,128)S(1)} fusion(bf16[1,24,128,1024]{3,2,1,0:T(8,128)(2,1)} %param.12, bf16[24,32,128]{2,1,0:T(8,128)(2,1)S(1)} %gather_fusion.1, f32[32,1024]{1,0:T(8,128)S(1)} %copy-done.1, f32[6,32,1024]{2,1,0:T(8,128)S(1)} %copy-done.2, bf16[24]{0:T(256)(128)(2,1)S(1)} %fusion.193), kind=kOutput, calls=%fused_computation.16 | convolution fusion | flops 201883648 | bytes 7143472 | tf_op jit(solution)/shard_map/dot_general | solution.py:197
  122.8 0.8 slice.528
  123.6 0.8 fusion.134
  124.4 27.0 %all-to-all-done.1 = bf16[32,6,1,32,128]{4,3,1,2,0:T(8,128)(2,1)S(1)} async-done(((bf16[32,6,1,32,128]{4,3,1,2,0:T(8,128)(2,1)}), bf16[32,6,1,32,128]{4,3,1,2,0:T(8,128)(2,1)S(1)}, u32[]{:S(2)}, u32[]{:S(2)}) %all-to-all-start.1) | async-done | bytes 1572896 | tf_op jit(solution)/shard_map/while/body/eval_jaxpr/all_to_all | solution.py:228
  151.4 1.8 gather_fusion.3
  153.2 1.4 multiply_bitcast_fusion
  154.6 0.8 copy.99
  155.4 4.3 %fusion.2 = f32[192,1024]{1,0:T(8,128)S(1)} fusion(bf16[3072,1024]{1,0:T(8,128)(2,1)} %bitcast.390, bf16[24,8,24,128]{3,2,1,0:T(8,128)(2,1)S(1)} %bitcast.394), kind=kOutput, calls=%fused_computation.6 | convolution fusion | flops 1207959552 | bytes 8257536 | tf_op jit(solution)/shard_map/while/body/eval_jaxpr/dot_general | solution.py:197
  166.4 13.6 %all_to_all.31 = f32[8,1,3072]{2,1,0:T(1,128)S(1)} all-to-all(f32[8,1,3072]{2,1,0:T(1,128)S(1)} %reshape.712), channel_id=1, replica_groups=mesh['grp_0'=4,'grp_1'=8,'node_0'=4,'node_1'=2] {'node_0','node_1'}, dimensions={0} | all-to-all | bytes 196608 | tf_op jit(solution)/shard_map/all_to_all | solution.py:57
  180.5 0.9 reduce.7
  181.7 13.9 %all_to_all.32 = f32[32,3,32]{2,1,0:T(4,128)S(1)} all-to-all(f32[32,3,32]{2,1,0:T(4,128)S(1)} %copy.102), channel_id=1, replica_groups=mesh['grp_0'=4,'grp_1'=8,'node_0'=4,'node_1'=2] {'grp_0','grp_1'}, dimensions={0} | all-to-all | bytes 24576 | tf_op jit(solution)/shard_map/all_to_all | solution.py:65
  195.6 12.1 %all_to_all.33 = f32[32,3,32]{2,1,0:T(4,128)S(1)} all-to-all(f32[32,3,32]{2,1,0:T(4,128)S(1)} %broadcast_in_dim.104), channel_id=1, replica_groups=mesh['grp_0'=4,'grp_1'=8,'node_0'=4,'node_1'=2] {'grp_0','grp_1'}, dimensions={0} | all-to-all | bytes 24576 | tf_op jit(solution)/shard_map/all_to_all | solution.py:35
  207.9 10.7 %all_to_all.34 = f32[8,1,3072]{2,1,0:T(1,128)S(1)} all-to-all(f32[8,1,3072]{2,1,0:T(1,128)S(1)} %reshape.714), channel_id=1, replica_groups=mesh['grp_0'=4,'grp_1'=8,'node_0'=4,'node_1'=2] {'node_0','node_1'}, dimensions={0} | all-to-all | bytes 196608 | tf_op jit(solution)/shard_map/all_to_all | solution.py:35
  218.6 0.9 reduce.8
  220.1 0.8 copy.105
  (123 shorter events, 10.6 us)
Async XLA Ops:
  0.6 163.5 %copy-start = (bf16[128,1024]{1,0:T(8,128)(2,1)S(1)}, bf16[128,1024]{1,0:T(8,128)(2,1)}, u32[]{:S(2)}) copy-start(bf16[128,1024]{1,0:T(8,128)(2,1)} %param.13) | copy-start | bytes 786436
  27.8 20.0 %copy-start.2 = (f32[6,32,1024]{2,1,0:T(8,128)S(1)}, f32[6,32,1024]{2,1,0:T(8,128)}, u32[]{:S(2)}) copy-start(f32[6,32,1024]{2,1,0:T(8,128)} %param.9) | copy-start | bytes 2359300
  35.5 70.1 %all-to-all-start = ((bf16[32,1,1,32,128]{4,3,2,1,0:T(8,128)(2,1)}), bf16[32,1,1,32,128]{4,3,2,1,0:T(8,128)(2,1)S(1)}, u32[]{:S(2)}, u32[]{:S(2)}) async-start(bf16[32,1,1,32,128]{4,3,2,1,0:T(8,128)(2,1)} %copy.94), calls=%async_computation | async-start | bytes 524288 | tf_op jit(solution)/shard_map/all_to_all | solution.py:218
  105.5 10.0 %copy-start.16 = (s32[256]{0:T(256)S(1)}, s32[256]{0:T(256)}, u32[]{:S(2)}) copy-start(s32[256]{0:T(256)} %param.17) | copy-start | bytes 3076
  105.5 10.6 %copy-start.15 = (s32[256,24]{0,1:T(8,128)S(1)}, s32[256,24]{0,1:T(8,128)}, u32[]{:S(2)}) copy-start(s32[256,24]{0,1:T(8,128)} %param.14) | copy-start | bytes 73732
  105.5 12.9 %copy-start.1 = (f32[32,1024]{1,0:T(8,128)S(1)}, f32[32,1024]{1,0:T(8,128)}, u32[]{:S(2)}) copy-start(f32[32,1024]{1,0:T(8,128)} %param.10) | copy-start | bytes 393220
  105.5 45.9 %all-to-all-start.1 = ((bf16[32,6,1,32,128]{4,3,1,2,0:T(8,128)(2,1)}), bf16[32,6,1,32,128]{4,3,1,2,0:T(8,128)(2,1)S(1)}, u32[]{:S(2)}, u32[]{:S(2)}) async-start(bf16[32,6,1,32,128]{4,3,1,2,0:T(8,128)(2,1)} %bitcast.28), calls=%async_computation.1 | async-start | bytes 3145728 | tf_op jit(solution)/shard_map/while/body/eval_jaxpr/all_to_all | solution.py:228
  118.5 4.2 %copy-start.3 = (f32[3,32,1024]{2,1,0:T(8,128)S(1)}, f32[3,32,1024]{2,1,0:T(8,128)}, u32[]{:S(2)}) copy-start(f32[3,32,1024]{2,1,0:T(8,128)} %slice.426) | copy-start | bytes 1179652
  118.5 4.2 %copy-start.6 = (f32[1,32,1024]{2,1,0:T(8,128)S(1)}, f32[1,32,1024]{2,1,0:T(8,128)}, u32[]{:S(2)}) copy-start(f32[1,32,1024]{2,1,0:T(8,128)} %get-tuple-element.83) | copy-start | bytes 393220
  118.5 4.2 %copy-start.8 = (f32[1,32,1024]{2,1,0:T(8,128)S(1)}, f32[1,32,1024]{2,1,0:T(8,128)}, u32[]{:S(2)}) copy-start(f32[1,32,1024]{2,1,0:T(8,128)} %get-tuple-element.84) | copy-start | bytes 393220
  122.6 1.0 copy-start.10
  155.4 4.4 %copy-start.4 = (f32[3,32,1024]{2,1,0:T(8,128)S(1)}, f32[3,32,1024]{2,1,0:T(8,128)}, u32[]{:S(2)}) copy-start(f32[3,32,1024]{2,1,0:T(8,128)} %slice.426) | copy-start | bytes 1179652
  155.4 4.4 %copy-start.5 = (f32[3,32,1024]{2,1,0:T(8,128)S(1)}, f32[3,32,1024]{2,1,0:T(8,128)}, u32[]{:S(2)}) copy-start(f32[3,32,1024]{2,1,0:T(8,128)} %slice.528) | copy-start | bytes 1179652
  155.4 4.4 %copy-start.7 = (f32[1,32,1024]{2,1,0:T(8,128)S(1)}, f32[1,32,1024]{2,1,0:T(8,128)}, u32[]{:S(2)}) copy-start(f32[1,32,1024]{2,1,0:T(8,128)} %get-tuple-element.83) | copy-start | bytes 393220
  155.4 4.4 %copy-start.9 = (f32[1,32,1024]{2,1,0:T(8,128)S(1)}, f32[1,32,1024]{2,1,0:T(8,128)}, u32[]{:S(2)}) copy-start(f32[1,32,1024]{2,1,0:T(8,128)} %get-tuple-element.84) | copy-start | bytes 393220
  155.4 4.4 %copy-start.11 = (f32[1,32,1024]{2,1,0:T(8,128)S(1)}, f32[1,32,1024]{2,1,0:T(8,128)}, u32[]{:S(2)}) copy-start(f32[1,32,1024]{2,1,0:T(8,128)} %copy-done.10) | copy-start | bytes 393220
  155.4 4.4 %copy-start.13 = (f32[1,32,1024]{2,1,0:T(8,128)S(1)}, f32[1,32,1024]{2,1,0:T(8,128)}, u32[]{:S(2)}) copy-start(f32[1,32,1024]{2,1,0:T(8,128)} %get-tuple-element.80) | copy-start | bytes 393220
  155.4 4.4 %copy-start.14 = (f32[1,32,1024]{2,1,0:T(8,128)S(1)}, f32[1,32,1024]{2,1,0:T(8,128)}, u32[]{:S(2)}) copy-start(f32[1,32,1024]{2,1,0:T(8,128)} %get-tuple-element.81) | copy-start | bytes 393220
  165.4 1.0 copy-start.12
where the time goes:
time: 222 us; the launch traced here: 221 us
  local copies, waits for them, and re-layouts  101 us (45%)
  blocking collectives  50.2 us (23%)
  waiting for transfers between devices  27 us (12%)
  starting transfers between devices  21 us (9%)
  other arithmetic  11 us (5%)
  matrix products  9.52 us (4%)
    gather x3, local copies, waits for them, and re-layouts, cut_piece(): lax.dynamic_slice(cycle, (slot_id, zero_index, start_id), (1, replicas, p...  47.9 us
    unnamed x44, local copies, waits for them, and re-layouts  27.2 us
    all_to_all x1, waiting for transfers between devices, one_batch(): lax.all_to_all(pack(cycle, in_times), GRP, split_axis=0, concat_axis=0, t...  27 us
    all_to_all x2, blocking collectives, from_everyone(): return lax.all_to_all(copies, axis, split_axis=0, concat_axis=0, tiled=True)  22.8 us
    dynamic_update_slice x1, local copies, waits for them, and re-layouts, store_fire(): lax.dynamic_update_slice(cycle, spike_density_result[None], (jnp.mod(step...  14.6 us
    all_to_all x1, blocking collectives, sum_in_two_steps(): lax.all_to_all(nearer, far, split_axis=0, concat_axis=0, tiled=True)  13.9 us
    all_to_all x1, blocking collectives, sent_and_summed(): blocks = lax.all_to_all(split_up(x, dim, length), axis, 0, 0, tiled=True)  13.6 us
    all_to_all x1, starting transfers between devices, body(): lax.all_to_all(pack(history, start_times), GRP, split_axis=0, concat_axis...  11.8 us
  transfers between devices with their start and end apart: 2, of which 1 were waited for; matrix products, arithmetic and copies ran while one was open for 31% of the time, Pallas kernels for 0%

commit v1 on v0

v1 whole, which is shorter than its diff:
```python
import functools

import jax
import jax.numpy as jnp
from jax import lax
from jax.experimental import pallas as pl
from jax.experimental.pallas import tpu as pltpu
from jax.sharding import Mesh
from jax.sharding import PartitionSpec as P

STEPS = 6
GRP = ("grp_0", "grp_1")
NODE = ("node_0", "node_1")
GRP_NODE = ("grp_0", "grp_1", "node_0", "node_1")

DT = 0.5


def firing(v):
    return 1.0 / (1.0 + jnp.exp(0.56 * (6.0 - v)))


def pack_kernel(codes, column, history, out, sems, *, owners, columns, piece):
    def parcel(g):
        code = codes[g * columns + column[0]]
        return pltpu.make_async_copy(
            history.at[pl.ds(code // 8, STEPS), :, pl.ds((code % 8) * piece, piece)],
            out.at[g],
            sems.at[g],
        )

    for g in range(owners):
        parcel(g).start()
    for g in range(owners):
        parcel(g).wait()


def pack_last_kernel(
    codes, column, history, initial, out, rows, fire, sems, row_sem, *, owners, columns, piece, cycle
):
    load = pltpu.make_async_copy(initial.at[pl.ds(1, 2)], rows, row_sem)
    load.start()
    load.wait()
    fire[...] = firing(rows[0] - rows[1]).astype(fire.dtype)

    def old(g, code):
        slot = jnp.minimum(code // 8 + STEPS, cycle - 1)
        return pltpu.make_async_copy(
            history.at[slot, :, pl.ds((code % 8) * piece, piece)], out.at[g], sems.at[g]
        )

    def new(g, code):
        return pltpu.make_async_copy(
            fire.at[:, pl.ds((code % 8) * piece, piece)], out.at[g], sems.at[g]
        )

    for g in range(owners):
        code = codes[g * columns + column[0]]

        @pl.when(code // 8 + STEPS >= cycle)
        def _():
            new(g, code).start()

        @pl.when(code // 8 + STEPS < cycle)
        def _():
            old(g, code).start()

    for g in range(owners):
        old(g, codes[g * columns + column[0]]).wait()


def fill_left(own, parcel, left, tiles, piece):
    rows = left.shape[0]
    for k in range(tiles):
        group = own[k]
        got = parcel[jnp.maximum(group, 0)].reshape(rows, piece)
        left[:, k * piece : (k + 1) * piece] = jnp.where(group >= 0, got, jnp.zeros_like(got))


def second_derivatives(y, noise, coupled):
    d3 = 3.25 * 0.1 * 0.005 * firing(y[1] - y[2]) - 2.0 * 0.1 * y[3] - 0.1 * 0.1 * y[0]
    drive = noise + 0.8 * 135.0 * 0.005 * firing(135.0 * y[0])
    if coupled is not None:
        drive = drive + 0.5 * coupled
    d4 = 3.25 * 0.1 * drive - 2.0 * 0.1 * y[4] - 0.1 * 0.1 * y[1]
    d5 = (
        22.0 * 0.05 * 0.25 * 135.0 * 0.005 * firing(0.25 * 135.0 * y[0])
        - 2.0 * 0.05 * y[5]
        - 0.05 * 0.05 * y[2]
    )
    return d3, d4, d5


def evolve_kernel(
    own, parcel, weights, initial, noise, lead, state, sensors, left, coupled, potential, *, tiles, piece
):
    replicas, nodes = noise.shape
    fill_left(own, parcel, left, tiles, piece)
    coupled[...] = jnp.dot(
        left[...], weights[...].reshape(tiles * piece, nodes), preferred_element_type=jnp.float32
    )
    width = 128

    def strip(i, carry):
        lanes = pl.ds(pl.multiple_of(i * width, width), width)
        y = [initial[r, :, lanes] for r in range(6)]
        p = noise[:, lanes]
        for s in range(STEPS):
            now = coupled[s * replicas : (s + 1) * replicas, lanes]
            then = None
            if s + 1 < STEPS:
                then = coupled[(s + 1) * replicas : (s + 2) * replicas, lanes]
            first = (y[3], y[4], y[5], *second_derivatives(y, p, now))
            mid = [a + DT * b for a, b in zip(y, first)]
            second = (mid[3], mid[4], mid[5], *second_derivatives(mid, p, then))
            y = [a + 0.5 * DT * (b + c) for a, b, c in zip(y, first, second)]
            potential[s * replicas : (s + 1) * replicas, lanes] = (y[1] - y[2]).astype(
                potential.dtype
            )
        for r in range(6):
            state[r, :, lanes] = y[r]
        return carry

    lax.fori_loop(0, nodes // width, strip, 0)
    sensors[...] = lax.dot_general(
        potential[...], lead[...], (((1,), (1,)), ((), ())), preferred_element_type=jnp.float32
    )


def finish_kernel(own, parcel, weights, before, after, left, row, sem_in, sem_out, *, tiles, piece):
    load = pltpu.make_async_copy(before.at[4], row, sem_in)
    load.start()
    fill_left(own, parcel, left, tiles, piece)
    nodes = row.shape[1]
    coupled = jnp.dot(
        left[...], weights[...].reshape(tiles * piece, nodes), preferred_element_type=jnp.float32
    )
    load.wait()
    row[...] = row[...] + 0.5 * DT * (3.25 * 0.1 * 0.5) * coupled
    store = pltpu.make_async_copy(row, after.at[4], sem_out)
    store.start()
    store.wait()


def to_all(x, axis):
    copies = jnp.broadcast_to(x, (lax.axis_size(axis), *x.shape))
    return lax.all_to_all(copies, axis, split_axis=0, concat_axis=0, tiled=True)


def total_of(x):
    columns = lax.axis_size(NODE)
    parts = x.reshape(columns, -1, x.shape[-1])
    mine = jnp.sum(lax.all_to_all(parts, NODE, split_axis=0, concat_axis=0, tiled=True), axis=0)
    mine = jnp.sum(to_all(mine, GRP), axis=0)
    return to_all(mine, NODE).reshape(x.shape)


def body(
    initial, afferent_noise_level, history, weights, lead_field, src_group, src_sub, delays, counts
):
    owners = lax.axis_size(GRP)
    columns = lax.axis_size(NODE)
    my_group = lax.axis_index(GRP)
    my_column = lax.axis_index(NODE)
    myself = my_group * columns + my_column
    cycle, replicas, nodes = history.shape
    tiles, piece = weights.shape[1:3]
    sensors_count = lead_field.shape[0]
    lanes = jnp.arange(tiles, dtype=jnp.int32)

    group_t, sub_t, delay_t = src_group.T, src_sub.T, delays.T
    live = lanes[:, None] < counts[None, :]
    codes = jnp.sum(
        jnp.where((group_t == my_group) & live, (cycle - delay_t) * 8 + sub_t, 0), axis=0
    )
    column = my_column.astype(jnp.int32).reshape(1)
    own_group = lax.dynamic_index_in_dim(group_t, myself, 1, False)
    own_count = lax.dynamic_index_in_dim(counts, myself, 0, False)
    own = jnp.where(lanes < own_count, own_group, -1)

    smem = pl.BlockSpec(memory_space=pltpu.SMEM)
    vmem = pl.BlockSpec(memory_space=pltpu.VMEM)
    anywhere = pl.BlockSpec(memory_space=pl.ANY)
    bf16, f32 = jnp.bfloat16, jnp.float32
    sizes = dict(owners=owners, columns=columns, piece=piece)

    packed = pl.pallas_call(
        functools.partial(pack_kernel, **sizes),
        out_shape=jax.ShapeDtypeStruct((owners, STEPS, replicas, piece), bf16),
        in_specs=[smem, smem, anywhere],
        out_specs=anywhere,
        scratch_shapes=[pltpu.SemaphoreType.DMA((owners,))],
        name="pack",
    )(codes, column, history)
    packed_last = pl.pallas_call(
        functools.partial(pack_last_kernel, cycle=cycle, **sizes),
        out_shape=jax.ShapeDtypeStruct((owners, replicas, piece), bf16),
        in_specs=[smem, smem, anywhere, anywhere],
        out_specs=anywhere,
        scratch_shapes=[
            pltpu.VMEM((2, replicas, nodes), f32),
            pltpu.VMEM((replicas, nodes), bf16),
            pltpu.SemaphoreType.DMA((owners,)),
            pltpu.SemaphoreType.DMA,
        ],
        name="pack_last",
    )(codes, column, history, initial)
    parcel = lax.all_to_all(packed, GRP, split_axis=0, concat_axis=0, tiled=True)
    parcel_last = lax.all_to_all(packed_last, GRP, split_axis=0, concat_axis=0, tiled=True)

    tile_stack = weights.reshape(tiles, piece, nodes)
    shape = dict(tiles=tiles, piece=piece)
    state, local = pl.pallas_call(
        functools.partial(evolve_kernel, **shape),
        out_shape=(
            jax.ShapeDtypeStruct(initial.shape, f32),
            jax.ShapeDtypeStruct((STEPS * replicas, sensors_count), f32),
        ),
        in_specs=[smem, vmem, vmem, vmem, vmem, vmem],
        out_specs=(vmem, vmem),
        scratch_shapes=[
            pltpu.VMEM((STEPS * replicas, tiles * piece), bf16),
            pltpu.VMEM((STEPS * replicas, nodes), f32),
            pltpu.VMEM((STEPS * replicas, nodes), bf16),
        ],
        name="evolve",
    )(own, parcel, tile_stack, initial, afferent_noise_level, lead_field)

    total = total_of(local)
    sensors = jnp.transpose(total.reshape(STEPS, replicas, sensors_count), (0, 2, 1))

    final_state = pl.pallas_call(
        functools.partial(finish_kernel, **shape),
        out_shape=jax.ShapeDtypeStruct(initial.shape, f32),
        in_specs=[smem, vmem, vmem, anywhere],
        out_specs=anywhere,
        scratch_shapes=[
            pltpu.VMEM((replicas, tiles * piece), bf16),
            pltpu.VMEM((replicas, nodes), f32),
            pltpu.SemaphoreType.DMA,
            pltpu.SemaphoreType.DMA,
        ],
        input_output_aliases={3: 0},
        name="finish",
    )(own, parcel_last, tile_stack, state)
    return final_state, sensors


def solution(mesh):
    finer = Mesh(mesh.devices.reshape(4, 8, 4, 2), GRP_NODE)
    placed = (
        P(None, None, GRP_NODE),
        P(None, GRP_NODE),
        P(None, None, GRP_NODE),
        P(GRP_NODE, None, None, None),
        P(None, GRP_NODE),
        P(),
        P(),
        P(),
        P(),
    )
    return jax.shard_map(
        body, mesh=finer, in_specs=placed, out_specs=(P(None, None, GRP_NODE), P()), check_vma=False
    )
```

time: 222 us -> 174 us (0.78)
  local copies, waits for them, and re-layouts: 101 us -> 4.02 us
  Pallas kernels: 0 us -> 74.7 us
  blocking collectives: 50.2 us -> 12.8 us
  waiting for transfers between devices: 27 us -> 45 us
  starting transfers between devices: 21 us -> 33.2 us
  matrix products: 9.52 us -> 0 us
  other arithmetic: 11 us -> 2.64 us
    pallas_call x0 -> x4, Pallas kernels: none -> 74.7 us  [the longest x1 49.9 us: body(): pl.pallas_call(functools.partial(pack_kernel, **sizes), out_shape=jax.Sha...]
    gather x5 -> x0, local copies, waits for them, and re-layouts: 50.3 us -> none  [the longest x3 47.9 us: cut_piece(): lax.dynamic_slice(cycle, (slot_id, zero_index, start_id), (1, replicas, p...]
    all_to_all x4 -> x1, blocking collectives: 50.2 us -> 12.8 us  [total_of(): lax.all_to_all(parts, NODE, split_axis=0, concat_axis=0, tiled=True)]
    unnamed x44 -> x9, local copies, waits for them, and re-layouts: 27.2 us -> 1.81 us
    all_to_all x2 -> x4, waiting for transfers between devices: 27 us -> 45 us  [the longest x1 34.9 us: body(): lax.all_to_all(packed, GRP, split_axis=0, concat_axis=0, tiled=True)]
    dynamic_update_slice x3 -> x0, local copies, waits for them, and re-layouts: 14.8 us -> none  [the longest x1 14.6 us: store_fire(): lax.dynamic_update_slice(cycle, spike_density_result[None], (jnp.mod(step...]
    all_to_all x2 -> x4, starting transfers between devices: 21 us -> 33.2 us  [the longest x2 12.4 us: to_all(): return lax.all_to_all(copies, axis, split_axis=0, concat_axis=0, tiled=True)]
    dot_general x8 -> x0, matrix products: 9.52 us -> none  [the longest x2 8.37 us: unpack(): jnp.dot(flattened, tile_stack, preferred_element_type=jnp.float32)]
  transfers between devices with their start and end apart: 2 -> 4, of which waited for: 1 -> 4; matrix products, arithmetic and copies ran while one was open for 31% -> 1% of each run, Pallas kernels for 0% -> 9%
where the time goes in v1:
time: 174 us; the launch traced here: 173 us
  Pallas kernels  74.7 us (43%)
  waiting for transfers between devices  45 us (26%)
  starting transfers between devices  33.2 us (19%)
  blocking collectives  12.8 us (7%)
  local copies, waits for them, and re-layouts  4.02 us (2%)
  other arithmetic  2.64 us (2%)
    pallas_call x1, Pallas kernels, body(): pl.pallas_call(functools.partial(pack_kernel, **sizes), out_shape=jax.Sha...  49.9 us
    all_to_all x1, waiting for transfers between devices, body(): lax.all_to_all(packed, GRP, split_axis=0, concat_axis=0, tiled=True)  34.9 us
    all_to_all x1, blocking collectives, total_of(): lax.all_to_all(parts, NODE, split_axis=0, concat_axis=0, tiled=True)  12.8 us
    all_to_all x2, starting transfers between devices, to_all(): return lax.all_to_all(copies, axis, split_axis=0, concat_axis=0, tiled=True)  12.4 us
    all_to_all x1, starting transfers between devices, body(): lax.all_to_all(packed, GRP, split_axis=0, concat_axis=0, tiled=True)  11.9 us
    pallas_call x1, Pallas kernels, body(): pl.pallas_call(functools.partial(pack_last_kernel, cycle=cycle, **sizes),...  11 us
    all_to_all x1, waiting for transfers between devices, body(): lax.all_to_all(packed_last, GRP, split_axis=0, concat_axis=0, tiled=True)  9.61 us
    pallas_call x1, Pallas kernels, body(): pl.pallas_call(functools.partial(evolve_kernel, **shape), out_shape=(jax....  9.01 us
  transfers between devices with their start and end apart: 4, of which 4 were waited for; matrix products, arithmetic and copies ran while one was open for 1% of the time, Pallas kernels for 9%

profile of v1, /device:TPU:1, one launch (start us, length us, event | category | flops | bytes accessed | tf_op | source)
XLA Modules:
  0.0 173.1 jit_solution(9326598165200216978)
XLA Ops:
  0.6 1.4 fusion.codes
  2.0 0.0 copy-start.3
  2.0 0.0 copy-start.2
  2.0 49.9 %pack.1 = bf16[32,6,32,128]{3,2,1,0:T(8,128)(2,1)} custom-call(s32[256]{0:T(256)} %fusion.codes, s32[1]{0:T(128)} %bitcast.3.column, bf16[64,32,1024]{2,1,0:T(8,128)(2,1)} %history.3), custom_call_target="tpu_custom_call" | custom-call | tf_op jit(solution)/shard_map/pack/pallas_call | solution.py:187
  51.9 11.9 %all-to-all-start.1 = ((bf16[32,6,32,128]{3,2,1,0:T(8,128)(2,1)}), bf16[32,6,32,128]{3,2,1,0:T(8,128)(2,1)S(1)}, u32[]{:S(2)}, u32[]{:S(2)}) async-start(bf16[32,6,32,128]{3,2,1,0:T(8,128)(2,1)} %pack.1), calls=%async_computation.1 | async-start | bytes 3145728 | tf_op jit(solution)/shard_map/all_to_all | solution.py:208
  63.8 0.0 copy-done.3
  63.8 0.6 dynamic_slice.6
  64.3 0.0 copy-done.2
  64.3 0.2 dynamic-slice_reduce_fusion
  64.5 1.2 compare_select_fusion.own
  65.8 34.9 %all-to-all-done.1.parcel = bf16[32,6,32,128]{3,2,1,0:T(8,128)(2,1)S(1)} async-done(((bf16[32,6,32,128]{3,2,1,0:T(8,128)(2,1)}), bf16[32,6,32,128]{3,2,1,0:T(8,128)(2,1)S(1)}, u32[]{:S(2)}, u32[]{:S(2)}) %all-to-all-start.1) | async-done | bytes 1572896 | tf_op jit(solution)/shard_map/all_to_all | solution.py:208
  100.7 0.0 copy-start
  100.7 1.2 copy-done
  101.8 9.0 %evolve.1 = (f32[6,32,1024]{2,1,0:T(8,128)}, f32[192,128]{1,0:T(8,128)}) custom-call(s32[24]{0:T(128)} %compare_select_fusion.own, bf16[32,6,32,128]{3,2,1,0:T(8,128)(2,1)} %copy-done, bf16[24,128,1024]{2,1,0:T(8,128)(2,1)} %bitcast.13, f32[6,32,1024]{2,1,0:T(8,128)} %initial.3, f32[32,1024]{1,0:T(8,128)} %noise.1, bf16[128,1024]{1,0:T(8,128)(2,1)} %lead.1), custom_call_target="tpu_custom_call" | custom-call | tf_op jit(solution)/shard_map/evolve/pallas_call | solution.py:213
  110.8 12.8 %all_to_all.25 = f32[8,24,128]{2,1,0:T(8,128)S(1)} all-to-all(f32[8,24,128]{2,1,0:T(8,128)} %bitcast.16), channel_id=1, replica_groups=mesh['grp_0'=4,'grp_1'=8,'node_0'=4,'node_1'=2] {'node_0','node_1'}, dimensions={0} | all-to-all | bytes 196608 | tf_op jit(solution)/shard_map/all_to_all | solution.py:153
  123.7 0.8 broadcast_in_dim.18
  124.4 5.3 %all-to-all-start.3 = ((f32[32,24,128]{2,1,0:T(8,128)}), f32[32,24,128]{2,1,0:T(8,128)S(1)}, u32[]{:S(2)}, u32[]{:S(2)}) async-start(f32[32,24,128]{2,1,0:T(8,128)} %broadcast_in_dim.18), calls=%async_computation.3 | async-start | bytes 786432 | tf_op jit(solution)/shard_map/all_to_all | solution.py:147
  129.8 11.0 %pack_last.1 = bf16[32,32,128]{2,1,0:T(8,128)(2,1)} custom-call(s32[256]{0:T(256)} %fusion.codes, s32[1]{0:T(128)} %bitcast.3.column, bf16[64,32,1024]{2,1,0:T(8,128)(2,1)} %history.3, f32[6,32,1024]{2,1,0:T(8,128)} %initial.3), custom_call_target="tpu_custom_call" | custom-call | tf_op jit(solution)/shard_map/pack_last/pallas_call | solution.py:195
  140.8 0.4 all-to-all-done.3
  141.2 8.9 %all-to-all-start = ((bf16[32,32,128]{2,1,0:T(8,128)(2,1)}), bf16[32,32,128]{2,1,0:T(8,128)(2,1)S(1)}, u32[]{:S(2)}, u32[]{:S(2)}) async-start(bf16[32,32,128]{2,1,0:T(8,128)(2,1)} %pack_last.1), calls=%async_computation | async-start | bytes 524288 | tf_op jit(solution)/shard_map/all_to_all | solution.py:209
  150.1 9.6 %all-to-all-done.parcel = bf16[32,32,128]{2,1,0:T(8,128)(2,1)S(1)} async-done(((bf16[32,32,128]{2,1,0:T(8,128)(2,1)}), bf16[32,32,128]{2,1,0:T(8,128)(2,1)S(1)}, u32[]{:S(2)}, u32[]{:S(2)}) %all-to-all-start) | async-done | bytes 262176 | tf_op jit(solution)/shard_map/all_to_all | solution.py:209
  159.7 0.0 copy-start.1
  159.7 0.7 broadcast_in_dim.19
  160.4 7.1 %all-to-all-start.4 = ((f32[8,24,128]{2,1,0:T(8,128)}), f32[8,24,128]{2,1,0:T(8,128)S(1)}, u32[]{:S(2)}, u32[]{:S(2)}) async-start(f32[8,24,128]{2,1,0:T(8,128)} %broadcast_in_dim.19), calls=%async_computation.4 | async-start | bytes 196608 | tf_op jit(solution)/shard_map/all_to_all | solution.py:147
  167.5 0.0 copy-done.1
  167.5 4.8 %finish.1 = f32[6,32,1024]{2,1,0:T(8,128)} custom-call(s32[24]{0:T(128)} %compare_select_fusion.own, bf16[32,32,128]{2,1,0:T(8,128)(2,1)} %copy-done.1, bf16[24,128,1024]{2,1,0:T(8,128)(2,1)} %bitcast.14, f32[6,32,1024]{2,1,0:T(8,128)} %get-tuple-element.4.before), custom_call_target="tpu_custom_call", output_to_operand_aliasing={{}: (3, {})} | custom-call | tf_op jit(solution)/shard_map/finish/pallas_call | solution.py:232
  172.3 0.2 all-to-all-done.4
  172.5 0.6 copy.14
  (2 shorter events, 0.1 us)
Async XLA Ops:
  2.0 61.8 %copy-start.3 = (s32[256]{0:T(256)S(1)}, s32[256]{0:T(256)}, u32[]{:S(2)}) copy-start(s32[256]{0:T(256)} %param.17) | copy-start | bytes 3076
  2.0 62.3 %copy-start.2 = (s32[256,24]{0,1:T(8,128)S(1)}, s32[256,24]{0,1:T(8,128)}, u32[]{:S(2)}) copy-start(s32[256,24]{0,1:T(8,128)} %param.14) | copy-start | bytes 73732
  51.9 48.8 %all-to-all-start.1 = ((bf16[32,6,32,128]{3,2,1,0:T(8,128)(2,1)}), bf16[32,6,32,128]{3,2,1,0:T(8,128)(2,1)S(1)}, u32[]{:S(2)}, u32[]{:S(2)}) async-start(bf16[32,6,32,128]{3,2,1,0:T(8,128)(2,1)} %pack.1), calls=%async_computation.1 | async-start | bytes 3145728 | tf_op jit(solution)/shard_map/all_to_all | solution.py:208
  100.7 1.2 copy-start
  124.4 16.7 %all-to-all-start.3 = ((f32[32,24,128]{2,1,0:T(8,128)}), f32[32,24,128]{2,1,0:T(8,128)S(1)}, u32[]{:S(2)}, u32[]{:S(2)}) async-start(f32[32,24,128]{2,1,0:T(8,128)} %broadcast_in_dim.18), calls=%async_computation.3 | async-start | bytes 786432 | tf_op jit(solution)/shard_map/all_to_all | solution.py:147
  141.2 18.5 %all-to-all-start = ((bf16[32,32,128]{2,1,0:T(8,128)(2,1)}), bf16[32,32,128]{2,1,0:T(8,128)(2,1)S(1)}, u32[]{:S(2)}, u32[]{:S(2)}) async-start(bf16[32,32,128]{2,1,0:T(8,128)(2,1)} %pack_last.1), calls=%async_computation | async-start | bytes 524288 | tf_op jit(solution)/shard_map/all_to_all | solution.py:209
  159.7 7.8 %copy-start.1 = (bf16[32,32,128]{2,1,0:T(8,128)(2,1)}, bf16[32,32,128]{2,1,0:T(8,128)(2,1)S(1)}, u32[]{:S(2)}) copy-start(bf16[32,32,128]{2,1,0:T(8,128)(2,1)S(1)} %all-to-all-done.parcel) | copy-start | bytes 786436
  160.4 12.1 %all-to-all-start.4 = ((f32[8,24,128]{2,1,0:T(8,128)}), f32[8,24,128]{2,1,0:T(8,128)S(1)}, u32[]{:S(2)}, u32[]{:S(2)}) async-start(f32[8,24,128]{2,1,0:T(8,128)} %broadcast_in_dim.19), calls=%async_computation.4 | async-start | bytes 196608 | tf_op jit(solution)/shard_map/all_to_all | solution.py:147

commit v2 on v1

--- a/solution.py
+++ b/solution.py
@@ -14,46 +14,41 @@
 GRP_NODE = ("grp_0", "grp_1", "node_0", "node_1")
 
 DT = 0.5
+MIB = 1 << 20
 
 
 def firing(v):
     return 1.0 / (1.0 + jnp.exp(0.56 * (6.0 - v)))
 
 
-def pack_kernel(codes, column, history, out, sems, *, owners, columns, piece):
-    def parcel(g):
-        code = codes[g * columns + column[0]]
+def pack_kernel(
+    codes, column, history, initial, out, last, rows, fire, sems, last_sems, row_sem, *, owners, columns, piece, cycle
+):
+    load = pltpu.make_async_copy(initial.at[pl.ds(1, 2)], rows, row_sem)
+    load.start()
+
+    def parcel(g, code):
         return pltpu.make_async_copy(
             history.at[pl.ds(code // 8, STEPS), :, pl.ds((code % 8) * piece, piece)],
             out.at[g],
             sems.at[g],
         )
 
-    for g in range(owners):
-        parcel(g).start()
-    for g in range(owners):
-        parcel(g).wait()
-
-
-def pack_last_kernel(
-    codes, column, history, initial, out, rows, fire, sems, row_sem, *, owners, columns, piece, cycle
-):
-    load = pltpu.make_async_copy(initial.at[pl.ds(1, 2)], rows, row_sem)
-    load.start()
-    load.wait()
-    fire[...] = firing(rows[0] - rows[1]).astype(fire.dtype)
-
     def old(g, code):
         slot = jnp.minimum(code // 8 + STEPS, cycle - 1)
         return pltpu.make_async_copy(
-            history.at[slot, :, pl.ds((code % 8) * piece, piece)], out.at[g], sems.at[g]
+            history.at[slot, :, pl.ds((code % 8) * piece, piece)], last.at[g], last_sems.at[g]
         )
 
     def new(g, code):
         return pltpu.make_async_copy(
-            fire.at[:, pl.ds((code % 8) * piece, piece)], out.at[g], sems.at[g]
-        )
-
+            fire.at[:, pl.ds((code % 8) * piece, piece)], last.at[g], last_sems.at[g]
+        )
+
+    for g in range(owners):
+        parcel(g, codes[g * columns + column[0]]).start()
+    load.wait()
+    fire[...] = firing(rows[0] - rows[1]).astype(fire.dtype)
     for g in range(owners):
         code = codes[g * columns + column[0]]
 
@@ -66,7 +61,9 @@
             old(g, code).start()
 
     for g in range(owners):
-        old(g, codes[g * columns + column[0]]).wait()
+        code = codes[g * columns + column[0]]
+        parcel(g, code).wait()
+        old(g, code).wait()
 
 
 def fill_left(own, parcel, left, tiles, piece):
@@ -92,19 +89,44 @@
 
 
 def evolve_kernel(
-    own, parcel, weights, initial, noise, lead, state, sensors, left, coupled, potential, *, tiles, piece
+    own, parcel, weights, initial, noise, lead, state, sensors,
+    stack, start, rate, gains, left, coupled, potential, sems, *, tiles, piece, pieces_at_once
 ):
     replicas, nodes = noise.shape
+    chunks = tiles // pieces_at_once
+    loads = [
+        pltpu.make_async_copy(
+            weights.at[pl.ds(i * pieces_at_once, pieces_at_once)],
+            stack.at[pl.ds(i * pieces_at_once, pieces_at_once)],
+            sems.at[i],
+        )
+        for i in range(chunks)
+    ]
+    others = [
+        pltpu.make_async_copy(initial, start, sems.at[chunks]),
+        pltpu.make_async_copy(noise, rate, sems.at[chunks + 1]),
+        pltpu.make_async_copy(lead, gains, sems.at[chunks + 2]),
+    ]
+    for load in loads + others:
+        load.start()
     fill_left(own, parcel, left, tiles, piece)
-    coupled[...] = jnp.dot(
-        left[...], weights[...].reshape(tiles * piece, nodes), preferred_element_type=jnp.float32
-    )
+    depth = pieces_at_once * piece
+    for i in range(chunks):
+        loads[i].wait()
+        part = jnp.dot(
+            left[:, i * depth : (i + 1) * depth],
+            stack[i * pieces_at_once : (i + 1) * pieces_at_once].reshape(depth, nodes),
+            preferred_element_type=jnp.float32,
+        )
+        coupled[...] = part if i == 0 else coupled[...] + part
+    for other in others:
+        other.wait()
     width = 128
 
     def strip(i, carry):
         lanes = pl.ds(pl.multiple_of(i * width, width), width)
-        y = [initial[r, :, lanes] for r in range(6)]
-        p = noise[:, lanes]
+        y = [start[r, :, lanes] for r in range(6)]
+        p = rate[:, lanes]
         for s in range(STEPS):
             now = coupled[s * replicas : (s + 1) * replicas, lanes]
             then = None
@@ -123,23 +145,23 @@
 
     lax.fori_loop(0, nodes // width, strip, 0)
     sensors[...] = lax.dot_general(
-        potential[...], lead[...], (((1,), (1,)), ((), ())), preferred_element_type=jnp.float32
-    )
-
-
-def finish_kernel(own, parcel, weights, before, after, left, row, sem_in, sem_out, *, tiles, piece):
-    load = pltpu.make_async_copy(before.at[4], row, sem_in)
+        potential[...], gains[...], (((1,), (1,)), ((), ())), preferred_element_type=jnp.float32
+    )
+
+
+def finish_kernel(own, parcel, weights, before, after, stack, left, sem, *, tiles, piece):
+    load = pltpu.make_async_copy(weights, stack, sem)
     load.start()
     fill_left(own, parcel, left, tiles, piece)
-    nodes = row.shape[1]
+    for r in (0, 1, 2, 3, 5):
+        after[r] = before[r]
+    load.wait()
     coupled = jnp.dot(
-        left[...], weights[...].reshape(tiles * piece, nodes), preferred_element_type=jnp.float32
-    )
-    load.wait()
-    row[...] = row[...] + 0.5 * DT * (3.25 * 0.1 * 0.5) * coupled
-    store = pltpu.make_async_copy(row, after.at[4], sem_out)
-    store.start()
-    store.wait()
+        left[...],
+        stack[...].reshape(tiles * piece, before.shape[2]),
+        preferred_element_type=jnp.float32,
+    )
+    after[4] = before[4] + 0.5 * DT * (3.25 * 0.1 * 0.5) * coupled
 
 
 def to_all(x, axis):
@@ -180,51 +202,62 @@
 
     smem = pl.BlockSpec(memory_space=pltpu.SMEM)
     vmem = pl.BlockSpec(memory_space=pltpu.VMEM)
-    anywhere = pl.BlockSpec(memory_space=pl.ANY)
+    far = pl.BlockSpec(memory_space=pltpu.HBM)
     bf16, f32 = jnp.bfloat16, jnp.float32
-    sizes = dict(owners=owners, columns=columns, piece=piece)
-
-    packed = pl.pallas_call(
-        functools.partial(pack_kernel, **sizes),
-        out_shape=jax.ShapeDtypeStruct((owners, STEPS, replicas, piece), bf16),
-        in_specs=[smem, smem, anywhere],
-        out_specs=anywhere,
-        scratch_shapes=[pltpu.SemaphoreType.DMA((owners,))],
-        name="pack",
-    )(codes, column, history)
-    packed_last = pl.pallas_call(
-        functools.partial(pack_last_kernel, cycle=cycle, **sizes),
-        out_shape=jax.ShapeDtypeStruct((owners, replicas, piece), bf16),
-        in_specs=[smem, smem, anywhere, anywhere],
-        out_specs=anywhere,
+
+    def near(x):
+        return pltpu.with_memory_space_constraint(x, pltpu.VMEM)
+
+    def outside(x):
+        return pltpu.with_memory_space_constraint(x, pltpu.HBM)
+
+
+    packed, packed_last = pl.pallas_call(
+        functools.partial(
+            pack_kernel, owners=owners, columns=columns, piece=piece, cycle=cycle
+        ),
+        out_shape=(
+            pltpu.VMEM((owners, STEPS, replicas, piece), bf16),
+            pltpu.VMEM((owners, replicas, piece), bf16),
+        ),
+        in_specs=[smem, smem, far, far],
+        out_specs=(vmem, vmem),
         scratch_shapes=[
             pltpu.VMEM((2, replicas, nodes), f32),
             pltpu.VMEM((replicas, nodes), bf16),
             pltpu.SemaphoreType.DMA((owners,)),
+            pltpu.SemaphoreType.DMA((owners,)),
             pltpu.SemaphoreType.DMA,
         ],
-        name="pack_last",
-    )(codes, column, history, initial)
+        compiler_params=pltpu.CompilerParams(vmem_limit_bytes=4 * MIB),
+        name="pack",
+    )(codes, column, outside(history), outside(initial))
     parcel = lax.all_to_all(packed, GRP, split_axis=0, concat_axis=0, tiled=True)
     parcel_last = lax.all_to_all(packed_last, GRP, split_axis=0, concat_axis=0, tiled=True)
 
-    tile_stack = weights.reshape(tiles, piece, nodes)
+    tile_stack = outside(weights.reshape(tiles, piece, nodes))
     shape = dict(tiles=tiles, piece=piece)
     state, local = pl.pallas_call(
-        functools.partial(evolve_kernel, **shape),
+        functools.partial(evolve_kernel, pieces_at_once=6, **shape),
         out_shape=(
-            jax.ShapeDtypeStruct(initial.shape, f32),
-            jax.ShapeDtypeStruct((STEPS * replicas, sensors_count), f32),
+            pltpu.VMEM(initial.shape, f32),
+            pltpu.VMEM((STEPS * replicas, sensors_count), f32),
         ),
-        in_specs=[smem, vmem, vmem, vmem, vmem, vmem],
+        in_specs=[smem, vmem, far, far, far, far],
         out_specs=(vmem, vmem),
         scratch_shapes=[
+            pltpu.VMEM(tile_stack.shape, bf16),
+            pltpu.VMEM(initial.shape, f32),
+            pltpu.VMEM(afferent_noise_level.shape, f32),
+            pltpu.VMEM(lead_field.shape, bf16),
             pltpu.VMEM((STEPS * replicas, tiles * piece), bf16),
             pltpu.VMEM((STEPS * replicas, nodes), f32),
             pltpu.VMEM((STEPS * replicas, nodes), bf16),
+            pltpu.SemaphoreType.DMA((tiles // 6 + 3,)),
         ],
+        compiler_params=pltpu.CompilerParams(vmem_limit_bytes=24 * MIB),
         name="evolve",
-    )(own, parcel, tile_stack, initial, afferent_noise_level, lead_field)
+    )(own, near(parcel), tile_stack, outside(initial), outside(afferent_noise_level), outside(lead_field))
 
     total = total_of(local)
     sensors = jnp.transpose(total.reshape(STEPS, replicas, sensors_count), (0, 2, 1))
@@ -232,17 +265,16 @@
     final_state = pl.pallas_call(
         functools.partial(finish_kernel, **shape),
         out_shape=jax.ShapeDtypeStruct(initial.shape, f32),
-        in_specs=[smem, vmem, vmem, anywhere],
-        out_specs=anywhere,
+        in_specs=[smem, vmem, far, vmem],
+        out_specs=vmem,
         scratch_shapes=[
+            pltpu.VMEM(tile_stack.shape, bf16),
             pltpu.VMEM((replicas, tiles * piece), bf16),
-            pltpu.VMEM((replicas, nodes), f32),
-            pltpu.SemaphoreType.DMA,
             pltpu.SemaphoreType.DMA,
         ],
-        input_output_aliases={3: 0},
+        compiler_params=pltpu.CompilerParams(vmem_limit_bytes=24 * MIB),
         name="finish",
-    )(own, parcel_last, tile_stack, state)
+    )(own, near(parcel_last), tile_stack, near(state))
     return final_state, sensors
 
 

time: 174 us -> 124 us (0.71)
  Pallas kernels: 74.7 us -> 18.1 us
  blocking collectives: 12.8 us -> 29.6 us
  starting transfers between devices: 33.2 us -> 26.5 us
  local copies, waits for them, and re-layouts: 4.02 us -> 2.1 us
    pallas_call x3 -> x2, Pallas kernels: 69.9 us -> 12.7 us  [the longest x1 7.21 us: body(): pl.pallas_call(functools.partial(evolve_kernel, pieces_at_once=6, **shape...]
    all_to_all x0 -> x1, blocking collectives: none -> 16.5 us  [to_all(): return lax.all_to_all(copies, axis, split_axis=0, concat_axis=0, tiled=True)]
    all_to_all x2 -> x1, starting transfers between devices: 12.4 us -> 6.96 us  [to_all(): return lax.all_to_all(copies, axis, split_axis=0, concat_axis=0, tiled=True)]
  transfers between devices with their start and end apart: 4 -> 3, of which waited for: 4 -> 2; matrix products, arithmetic and copies ran while one was open for 1% -> 1% of each run, Pallas kernels for 9% -> 4%
where the time goes in v2:
time: 124 us
  waiting for transfers between devices  44.9 us (36%)
  blocking collectives  29.6 us (24%)
  starting transfers between devices  26.5 us (21%)
  Pallas kernels  18.1 us (15%)
  local copies, waits for them, and re-layouts  2.1 us (2%)
  other arithmetic  1.52 us (1%)
    all_to_all x1, waiting for transfers between devices, body(): lax.all_to_all(packed, GRP, split_axis=0, concat_axis=0, tiled=True)  35.3 us
    all_to_all x1, blocking collectives, to_all(): return lax.all_to_all(copies, axis, split_axis=0, concat_axis=0, tiled=True)  16.5 us
    all_to_all x1, blocking collectives, total_of(): lax.all_to_all(parts, NODE, split_axis=0, concat_axis=0, tiled=True)  13.1 us
    all_to_all x1, starting transfers between devices, body(): lax.all_to_all(packed, GRP, split_axis=0, concat_axis=0, tiled=True)  11.8 us
    all_to_all x1, waiting for transfers between devices, body(): lax.all_to_all(packed_last, GRP, split_axis=0, concat_axis=0, tiled=True)  9.6 us
    all_to_all x1, starting transfers between devices, body(): lax.all_to_all(packed_last, GRP, split_axis=0, concat_axis=0, tiled=True)  7.7 us
    pallas_call x1, Pallas kernels, body(): pl.pallas_call(functools.partial(evolve_kernel, pieces_at_once=6, **shape...  7.21 us
    all_to_all x1, starting transfers between devices, to_all(): return lax.all_to_all(copies, axis, split_axis=0, concat_axis=0, tiled=True)  6.96 us
  transfers between devices with their start and end apart: 3, of which 2 were waited for; matrix products, arithmetic and copies ran while one was open for 1% of the time, Pallas kernels for 4%

profile of v2, /device:TPU:1, one launch (start us, length us, event | category | flops | bytes accessed | tf_op | source)
XLA Modules:
  0.0 123.5 jit_solution(17874021362439392624)
XLA Ops:
  0.6 0.0 copy-start.1
  0.6 0.0 copy-start
  0.7 0.8 fusion.codes
  1.5 5.5 %pack.1 = (bf16[32,6,32,128]{3,2,1,0:T(8,128)(2,1)}, bf16[32,32,128]{2,1,0:T(8,128)(2,1)}) custom-call(s32[256]{0:T(256)S(1)} %fusion.codes, s32[1]{0:T(128)} %bitcast.3.column, bf16[64,32,1024]{2,1,0:T(8,128)(2,1)} %history.1, f32[6,32,1024]{2,1,0:T(8,128)} %initial.3), custom_call_target="tpu_custom_call" | custom-call | tf_op jit(solution)/shard_map/pack/pallas_call | solution.py:215
  7.0 11.8 %all-to-all-start.1 = ((bf16[32,6,32,128]{3,2,1,0:T(8,128)(2,1)}), bf16[32,6,32,128]{3,2,1,0:T(8,128)(2,1)S(1)}, u32[]{:S(2)}, u32[]{:S(2)}) async-start(bf16[32,6,32,128]{3,2,1,0:T(8,128)(2,1)} %get-tuple-element.7), calls=%async_computation.1 | async-start | bytes 3145728 | tf_op jit(solution)/shard_map/all_to_all | solution.py:235
  18.8 0.0 copy-done.1
  18.9 0.6 dynamic_slice.6
  19.4 0.0 copy-done
  19.4 0.2 dynamic-slice_reduce_fusion
  19.6 0.7 compare_select_fusion.own
  20.3 35.3 %all-to-all-done.1.parcel = bf16[32,6,32,128]{3,2,1,0:T(8,128)(2,1)S(1)} async-done(((bf16[32,6,32,128]{3,2,1,0:T(8,128)(2,1)}), bf16[32,6,32,128]{3,2,1,0:T(8,128)(2,1)S(1)}, u32[]{:S(2)}, u32[]{:S(2)}) %all-to-all-start.1) | async-done | bytes 1572896 | tf_op jit(solution)/shard_map/all_to_all | solution.py:235
  55.6 7.2 %evolve.1 = (f32[6,32,1024]{2,1,0:T(8,128)S(1)}, f32[192,128]{1,0:T(8,128)S(1)}) custom-call(s32[24]{0:T(128)S(1)} %compare_select_fusion.own, bf16[32,6,32,128]{3,2,1,0:T(8,128)(2,1)S(1)} %all-to-all-done.1.parcel, bf16[24,128,1024]{2,1,0:T(8,128)(2,1)} %bitcast.14, f32[6,32,1024]{2,1,0:T(8,128)} %initial.3, f32[32,1024]{1,0:T(8,128)} %noise.1, ...), custom_call_target="tpu_custom_call" | custom-call | tf_op jit(solution)/shard_map/evolve/pallas_call | solution.py:240
  62.8 13.1 %all_to_all.25 = f32[8,24,128]{2,1,0:T(8,128)S(1)} all-to-all(f32[8,24,128]{2,1,0:T(8,128)S(1)} %bitcast.13), channel_id=1, replica_groups=mesh['grp_0'=4,'grp_1'=8,'node_0'=4,'node_1'=2] {'node_0','node_1'}, dimensions={0} | all-to-all | bytes 196608 | tf_op jit(solution)/shard_map/all_to_all | solution.py:175
  75.9 16.5 %all_to_all.26 = f32[32,24,128]{2,1,0:T(8,128)S(1)} all-to-all(f32[32,24,128]{2,1,0:T(8,128)S(1)} %broadcast_in_dim.18), channel_id=1, replica_groups=mesh['grp_0'=4,'grp_1'=8,'node_0'=4,'node_1'=2] {'grp_0','grp_1'}, dimensions={0} | all-to-all | bytes 786432 | tf_op jit(solution)/shard_map/all_to_all | solution.py:169
  92.5 7.7 %all-to-all-start = ((bf16[32,32,128]{2,1,0:T(8,128)(2,1)}), bf16[32,32,128]{2,1,0:T(8,128)(2,1)S(1)}, u32[]{:S(2)}, u32[]{:S(2)}) async-start(bf16[32,32,128]{2,1,0:T(8,128)(2,1)} %get-tuple-element.6), calls=%async_computation | async-start | bytes 524288 | tf_op jit(solution)/shard_map/all_to_all | solution.py:236
  100.2 9.6 %all-to-all-done.parcel = bf16[32,32,128]{2,1,0:T(8,128)(2,1)S(1)} async-done(((bf16[32,32,128]{2,1,0:T(8,128)(2,1)}), bf16[32,32,128]{2,1,0:T(8,128)(2,1)S(1)}, u32[]{:S(2)}, u32[]{:S(2)}) %all-to-all-start) | async-done | bytes 262176 | tf_op jit(solution)/shard_map/all_to_all | solution.py:236
  109.8 0.6 broadcast_in_dim.19
  110.5 7.0 %all-to-all-start.4 = ((f32[8,24,128]{2,1,0:T(8,128)}), f32[8,24,128]{2,1,0:T(8,128)S(1)}, u32[]{:S(2)}, u32[]{:S(2)}) async-start(f32[8,24,128]{2,1,0:T(8,128)} %broadcast_in_dim.19), calls=%async_computation.4 | async-start | bytes 196608 | tf_op jit(solution)/shard_map/all_to_all | solution.py:169
  117.4 5.4 %finish.1 = f32[6,32,1024]{2,1,0:T(8,128)} custom-call(s32[24]{0:T(128)S(1)} %compare_select_fusion.own, bf16[32,32,128]{2,1,0:T(8,128)(2,1)S(1)} %all-to-all-done.parcel, bf16[24,128,1024]{2,1,0:T(8,128)(2,1)} %bitcast.15, f32[6,32,1024]{2,1,0:T(8,128)S(1)} %get-tuple-element.8.before), custom_call_target="tpu_custom_call" | custom-call | tf_op jit(solution)/shard_map/finish/pallas_call | solution.py:265
  122.8 0.0 all-to-all-done.4
  122.9 0.6 copy.12
  (3 shorter events, 0.1 us)
Async XLA Ops:
  0.6 18.2 %copy-start.1 = (s32[256]{0:T(256)S(1)}, s32[256]{0:T(256)}, u32[]{:S(2)}) copy-start(s32[256]{0:T(256)} %param.17) | copy-start | bytes 3076
  0.6 18.8 %copy-start = (s32[256,24]{0,1:T(8,128)S(1)}, s32[256,24]{0,1:T(8,128)}, u32[]{:S(2)}) copy-start(s32[256,24]{0,1:T(8,128)} %param.14) | copy-start | bytes 73732
  7.0 48.6 %all-to-all-start.1 = ((bf16[32,6,32,128]{3,2,1,0:T(8,128)(2,1)}), bf16[32,6,32,128]{3,2,1,0:T(8,128)(2,1)S(1)}, u32[]{:S(2)}, u32[]{:S(2)}) async-start(bf16[32,6,32,128]{3,2,1,0:T(8,128)(2,1)} %get-tuple-element.7), calls=%async_computation.1 | async-start | bytes 3145728 | tf_op jit(solution)/shard_map/all_to_all | solution.py:235
  92.5 17.4 %all-to-all-start = ((bf16[32,32,128]{2,1,0:T(8,128)(2,1)}), bf16[32,32,128]{2,1,0:T(8,128)(2,1)S(1)}, u32[]{:S(2)}, u32[]{:S(2)}) async-start(bf16[32,32,128]{2,1,0:T(8,128)(2,1)} %get-tuple-element.6), calls=%async_computation | async-start | bytes 524288 | tf_op jit(solution)/shard_map/all_to_all | solution.py:236
  110.5 12.4 %all-to-all-start.4 = ((f32[8,24,128]{2,1,0:T(8,128)}), f32[8,24,128]{2,1,0:T(8,128)S(1)}, u32[]{:S(2)}, u32[]{:S(2)}) async-start(f32[8,24,128]{2,1,0:T(8,128)} %broadcast_in_dim.19), calls=%async_computation.4 | async-start | bytes 196608 | tf_op jit(solution)/shard_map/all_to_all | solution.py:169

commit v3 on v2

v3 whole, which is shorter than its diff:
```python
import functools

import jax
import jax.numpy as jnp
from jax import lax
from jax.experimental import pallas as pl
from jax.experimental.pallas import tpu as pltpu
from jax.sharding import Mesh
from jax.sharding import PartitionSpec as P

STEPS = 6
TIMES = STEPS + 1
GRP = ("grp_0", "grp_1")
NODE = ("node_0", "node_1")
GRP_NODE = ("grp_0", "grp_1", "node_0", "node_1")

DT = 0.5
MIB = 1 << 20


def firing(v):
    return 1.0 / (1.0 + jnp.exp(0.56 * (6.0 - v)))


def pack_kernel(
    codes, column, history, initial, out, parts, rows, fire, gets, puts, row_sem, *, owners, columns, piece, cycle
):
    replicas = fire.shape[0]
    load = pltpu.make_async_copy(initial.at[pl.ds(1, 2)], rows, row_sem)
    load.start()

    def code_of(g):
        return codes[g * columns + column[0]]

    def get(g):
        start = jnp.minimum((code_of(g) >> 3), cycle - TIMES)
        sub = (code_of(g) & 7) * piece
        return pltpu.make_async_copy(
            history.at[pl.ds(start, TIMES), :, pl.ds(sub, piece)], parts.at[g], gets.at[g]
        )

    def put(g):
        return pltpu.make_async_copy(parts.at[g], out.at[g], puts.at[g])

    def reaches(g):
        return (code_of(g) >> 3) + TIMES > cycle

    for g in range(owners):
        get(g).start()
    load.wait()
    fire[...] = firing(rows[0] - rows[1]).astype(fire.dtype)
    for g in range(owners):
        get(g).wait()

        @pl.when(reaches(g))
        def _():
            sub = pl.multiple_of((code_of(g) & 7) * piece, piece)
            for t in range(TIMES - 1):
                parts[g, t] = parts[g, t + 1]
            parts[g, TIMES - 1] = fire[:, pl.ds(sub, piece)]

        put(g).start()
    for g in range(owners):
        put(g).wait()


def fill_left(own, parcel, left, tiles, piece):
    rows = left.shape[0]
    for k in range(tiles):
        group = own[k]
        got = parcel[jnp.maximum(group, 0)].reshape(rows, piece)
        left[:, k * piece : (k + 1) * piece] = jnp.where(group >= 0, got, jnp.zeros_like(got))


Q = 0.5 * DT * DT
G0 = Q * 3.25 * 0.1 * 0.005 * 0.5
G1 = Q * 3.25 * 0.1 * 0.8 * 135.0 * 0.005 * 0.5
G2 = Q * 22.0 * 0.05 * 0.25 * 135.0 * 0.005 * 0.5
DRIVE = Q * 3.25 * 0.1


def increments(y, z, drive):
    steep = (0.28 * 135.0) * y[0]
    t0 = jnp.tanh(0.28 * (y[1] - y[2]) - 1.68)
    t1 = jnp.tanh(steep - 1.68)
    t2 = jnp.tanh(0.25 * steep - 1.68)
    return (
        G0 * t0 + G0 - (Q * 0.2 / DT) * z[0] - (Q * 0.01) * y[0],
        G1 * t1 + drive - (Q * 0.2 / DT) * z[1] - (Q * 0.01) * y[1],
        G2 * t2 + G2 - (Q * 0.1 / DT) * z[2] - (Q * 0.0025) * y[2],
    )


def evolve_kernel(
    own, parcel, weights, initial, noise, lead, state, sensors,
    stack, start, rate, gains, left, coupled, potential, sems, *, tiles, piece, width, ahead
):
    replicas, nodes = noise.shape
    chunks = nodes // width
    loads = [
        pltpu.make_async_copy(weights.at[:, :, pl.ds(i * width, width)], stack.at[i], sems.at[i])
        for i in range(chunks)
    ]
    others = [
        pltpu.make_async_copy(initial, start, sems.at[chunks]),
        pltpu.make_async_copy(noise, rate, sems.at[chunks + 1]),
        pltpu.make_async_copy(lead, gains, sems.at[chunks + 2]),
    ]
    loads[0].start()
    for other in others:
        other.start()
    for load in loads[1:ahead]:
        load.start()
    fill_left(own, parcel, left, tiles, piece)
    lane = width

    def strip(i, carry):
        lanes = pl.ds(pl.multiple_of(i * lane, lane), lane)
        y = [start[r, :, lanes] for r in range(3)]
        z = [DT * start[r, :, lanes] for r in range(3, 6)]
        noisy = DRIVE * rate[:, lanes] + G1
        drives = [
            noisy + (0.5 * DRIVE) * coupled[t * replicas : (t + 1) * replicas, lanes]
            for t in range(2)
        ]
        for s in range(STEPS):
            w = increments(y, z, drives[s])
            y = [a + b for a, b in zip(y, z)]
            part = [a + b for a, b in zip(z, w)]
            second = increments(y, [a + b for a, b in zip(part, w)], drives[s + 1])
            y = [a + b for a, b in zip(y, w)]
            z = [a + b for a, b in zip(part, second)]
            potential[s * replicas : (s + 1) * replicas, lanes] = (y[1] - y[2]).astype(
                potential.dtype
            )
            if s + 2 < TIMES:
                drives.append(
                    noisy
                    + (0.5 * DRIVE) * coupled[(s + 2) * replicas : (s + 3) * replicas, lanes]
                )
        for r in range(3):
            state[r, :, lanes] = y[r]
            state[r + 3, :, lanes] = (1.0 / DT) * z[r]
        return carry

    for i in range(chunks):
        loads[i].wait()
        if i + ahead < chunks:
            loads[i + ahead].start()
        coupled[:, i * width : (i + 1) * width] = jnp.dot(
            left[...],
            stack[i].reshape(tiles * piece, width),
            preferred_element_type=jnp.float32,
        )
        if i == 0:
            for other in others:
                other.wait()
        lax.fori_loop(i * width // lane, (i + 1) * width // lane, strip, 0)
    sensors[...] = lax.dot_general(
        potential[...], gains[...], (((1,), (1,)), ((), ())), preferred_element_type=jnp.float32
    )


def to_all(x, axis):
    copies = jnp.broadcast_to(x, (lax.axis_size(axis), *x.shape))
    return lax.all_to_all(copies, axis, split_axis=0, concat_axis=0, tiled=True)


def total_of(x):
    columns = lax.axis_size(NODE)
    parts = x.reshape(columns, -1, x.shape[-1])
    mine = jnp.sum(lax.all_to_all(parts, NODE, split_axis=0, concat_axis=0, tiled=True), axis=0)
    mine = jnp.sum(to_all(mine, GRP), axis=0)
    return to_all(mine, NODE).reshape(x.shape)


def body(
    initial, afferent_noise_level, history, weights, lead_field, src_group, src_sub, delays, counts
):
    owners = lax.axis_size(GRP)
    columns = lax.axis_size(NODE)
    my_group = lax.axis_index(GRP)
    my_column = lax.axis_index(NODE)
    myself = my_group * columns + my_column
    cycle, replicas, nodes = history.shape
    tiles, piece = weights.shape[1:3]
    sensors_count = lead_field.shape[0]
    lanes = jnp.arange(tiles, dtype=jnp.int32)

    group_t, sub_t, delay_t = src_group.T, src_sub.T, delays.T
    live = lanes[:, None] < counts[None, :]
    codes = jnp.sum(
        jnp.where((group_t == my_group) & live, (cycle - delay_t) * 8 + sub_t, 0), axis=0
    )
    column = my_column.astype(jnp.int32).reshape(1)
    mine = (jnp.arange(counts.shape[0], dtype=jnp.int32) == myself)[None, :] & live
    own = jnp.sum(jnp.where(mine, group_t + 1, 0), axis=1) - 1

    smem = pl.BlockSpec(memory_space=pltpu.SMEM)
    vmem = pl.BlockSpec(memory_space=pltpu.VMEM)
    far = pl.BlockSpec(memory_space=pltpu.HBM)
    bf16, f32 = jnp.bfloat16, jnp.float32

    def near(x):
        return pltpu.with_memory_space_constraint(x, pltpu.VMEM)

    def outside(x):
        return pltpu.with_memory_space_constraint(x, pltpu.HBM)


    packed = pl.pallas_call(
        functools.partial(
            pack_kernel, owners=owners, columns=columns, piece=piece, cycle=cycle
        ),
        out_shape=pltpu.HBM((owners, TIMES, replicas, piece), bf16),
        in_specs=[smem, smem, far, far],
        out_specs=far,
        scratch_shapes=[
            pltpu.VMEM((owners, TIMES, replicas, piece), bf16),
            pltpu.VMEM((2, replicas, nodes), f32),
            pltpu.VMEM((replicas, nodes), bf16),
            pltpu.SemaphoreType.DMA((owners,)),
            pltpu.SemaphoreType.DMA((owners,)),
            pltpu.SemaphoreType.DMA,
        ],
        compiler_params=pltpu.CompilerParams(vmem_limit_bytes=8 * MIB),
        name="pack",
    )(codes, column, outside(history), outside(initial))
    parcel = lax.all_to_all(packed, GRP, split_axis=0, concat_axis=0, tiled=True)

    tile_stack = outside(weights.reshape(tiles, piece, nodes))
    width = 512
    state, local = pl.pallas_call(
        functools.partial(evolve_kernel, tiles=tiles, piece=piece, width=width, ahead=2),
        out_shape=(
            pltpu.VMEM(initial.shape, f32),
            pltpu.VMEM((STEPS * replicas, sensors_count), f32),
        ),
        in_specs=[smem, vmem, far, far, far, far],
        out_specs=(vmem, vmem),
        scratch_shapes=[
            pltpu.VMEM((nodes // width, tiles, piece, width), bf16),
            pltpu.VMEM(initial.shape, f32),
            pltpu.VMEM(afferent_noise_level.shape, f32),
            pltpu.VMEM(lead_field.shape, bf16),
            pltpu.VMEM((TIMES * replicas, tiles * piece), bf16),
            pltpu.VMEM((TIMES * replicas, nodes), f32),
            pltpu.VMEM((STEPS * replicas, nodes), bf16),
            pltpu.SemaphoreType.DMA((nodes // width + 3,)),
        ],
        compiler_params=pltpu.CompilerParams(vmem_limit_bytes=24 * MIB),
        name="evolve",
    )(own, near(parcel), tile_stack, outside(initial), outside(afferent_noise_level), outside(lead_field))

    total = total_of(local)
    sensors = jnp.transpose(total.reshape(STEPS, replicas, sensors_count), (0, 2, 1))
    return state, sensors


def solution(mesh):
    finer = Mesh(mesh.devices.reshape(4, 8, 4, 2), GRP_NODE)
    placed = (
        P(None, None, GRP_NODE),
        P(None, GRP_NODE),
        P(None, None, GRP_NODE),
        P(GRP_NODE, None, None, None),
        P(None, GRP_NODE),
        P(),
        P(),
        P(),
        P(),
    )
    return jax.shard_map(
        body, mesh=finer, in_specs=placed, out_specs=(P(None, None, GRP_NODE), P()), check_vma=False
    )
```

time: 124 us -> 110 us (0.89)
  Pallas kernels: 18.1 us -> 10.6 us
  starting transfers between devices: 26.5 us -> 19.4 us
  waiting for transfers between devices: 44.9 us -> 47.1 us
    all_to_all x1 -> x0, waiting for transfers between devices: 9.6 us -> none  [body(): lax.all_to_all(packed_last, GRP, split_axis=0, concat_axis=0, tiled=True)]
    all_to_all x1, waiting for transfers between devices: 35.3 us -> 43 us  [body(): lax.all_to_all(packed, GRP, split_axis=0, concat_axis=0, tiled=True)]
    all_to_all x1 -> x0, starting transfers between devices: 7.7 us -> none  [body(): lax.all_to_all(packed_last, GRP, split_axis=0, concat_axis=0, tiled=True)]
    pallas_call x2 -> x1, Pallas kernels: 12.6 us -> 6.33 us  [body(): pl.pallas_call(functools.partial(evolve_kernel, tiles=tiles, piece=piece,...]
    all_to_all x1, waiting for transfers between devices: 0.01 us -> 4.12 us  [to_all(): return lax.all_to_all(copies, axis, split_axis=0, concat_axis=0, tiled=True)]
    all_to_all x1, blocking collectives: 13.1 us -> 11.8 us  [total_of(): lax.all_to_all(parts, NODE, split_axis=0, concat_axis=0, tiled=True)]
    pallas_call x1, Pallas kernels: 5.53 us -> 4.28 us  [body(): pl.pallas_call(functools.partial(pack_kernel, owners=owners, columns=colu...]
  transfers between devices with their start and end apart: 3 -> 2, of which waited for: 2 -> 2; matrix products, arithmetic and copies ran while one was open for 1% -> 1% of each run, Pallas kernels for 4% -> 0%
where the time goes in v3:
time: 110 us
  waiting for transfers between devices  47.1 us (43%)
  blocking collectives  28.6 us (26%)
  starting transfers between devices  19.4 us (18%)
  Pallas kernels  10.6 us (10%)
  local copies, waits for them, and re-layouts  2.2 us (2%)
    all_to_all x1, waiting for transfers between devices, body(): lax.all_to_all(packed, GRP, split_axis=0, concat_axis=0, tiled=True)  43 us
    all_to_all x1, blocking collectives, to_all(): return lax.all_to_all(copies, axis, split_axis=0, concat_axis=0, tiled=True)  16.8 us
    all_to_all x1, starting transfers between devices, body(): lax.all_to_all(packed, GRP, split_axis=0, concat_axis=0, tiled=True)  12 us
    all_to_all x1, blocking collectives, total_of(): lax.all_to_all(parts, NODE, split_axis=0, concat_axis=0, tiled=True)  11.8 us
    all_to_all x1, starting transfers between devices, to_all(): return lax.all_to_all(copies, axis, split_axis=0, concat_axis=0, tiled=True)  7.37 us
    pallas_call x1, Pallas kernels, body(): pl.pallas_call(functools.partial(evolve_kernel, tiles=tiles, piece=piece,...  6.33 us
    pallas_call x1, Pallas kernels, body(): pl.pallas_call(functools.partial(pack_kernel, owners=owners, columns=colu...  4.28 us
    all_to_all x1, waiting for transfers between devices, to_all(): return lax.all_to_all(copies, axis, split_axis=0, concat_axis=0, tiled=True)  4.12 us
  transfers between devices with their start and end apart: 2, of which 2 were waited for; matrix products, arithmetic and copies ran while one was open for 1% of the time, Pallas kernels for 0%

profile of v3, /device:TPU:1, one launch (start us, length us, event | category | flops | bytes accessed | tf_op | source)
XLA Modules:
  0.0 109.6 jit_solution(15428586214553572987)
XLA Ops:
  0.7 0.9 fusion
  1.6 4.3 %pack.1 = bf16[32,7,32,128]{3,2,1,0:T(8,128)(2,1)} custom-call(s32[256]{0:T(256)S(1)} %get-tuple-element.6.codes, s32[1]{0:T(128)} %bitcast.3.column, bf16[64,32,1024]{2,1,0:T(8,128)(2,1)} %history.1, f32[6,32,1024]{2,1,0:T(8,128)} %initial.3), custom_call_target="tpu_custom_call" | custom-call | tf_op jit(solution)/shard_map/pack/pallas_call | solution.py:211
  5.9 12.0 %all-to-all-start = ((bf16[32,7,32,128]{3,2,1,0:T(8,128)(2,1)}), bf16[32,7,32,128]{3,2,1,0:T(8,128)(2,1)S(1)}, u32[]{:S(2)}, u32[]{:S(2)}) async-start(bf16[32,7,32,128]{3,2,1,0:T(8,128)(2,1)} %pack.1), calls=%async_computation | async-start | bytes 3670016 | tf_op jit(solution)/shard_map/all_to_all | solution.py:229
  17.9 43.0 %all-to-all-done.parcel = bf16[32,7,32,128]{3,2,1,0:T(8,128)(2,1)S(1)} async-done(((bf16[32,7,32,128]{3,2,1,0:T(8,128)(2,1)}), bf16[32,7,32,128]{3,2,1,0:T(8,128)(2,1)S(1)}, u32[]{:S(2)}, u32[]{:S(2)}) %all-to-all-start) | async-done | bytes 1835040 | tf_op jit(solution)/shard_map/all_to_all | solution.py:229
  60.9 6.3 %evolve.1 = (f32[6,32,1024]{2,1,0:T(8,128)S(1)}, f32[192,128]{1,0:T(8,128)S(1)}) custom-call(s32[24]{0:T(128)S(1)} %broadcast_add_fusion.own, bf16[32,7,32,128]{3,2,1,0:T(8,128)(2,1)S(1)} %all-to-all-done.parcel, bf16[24,128,1024]{2,1,0:T(8,128)(2,1)} %bitcast.17, f32[6,32,1024]{2,1,0:T(8,128)} %initial.3, f32[32,1024]{1,0:T(8,128)} %noise.1, ...), custom_call_target="tpu_custom_call" | custom-call | tf_op jit(solution)/shard_map/evolve/pallas_call | solution.py:233
  67.3 11.8 %all_to_all.20 = f32[8,24,128]{2,1,0:T(8,128)S(1)} all-to-all(f32[8,24,128]{2,1,0:T(8,128)S(1)} %bitcast.16), channel_id=1, replica_groups=mesh['grp_0'=4,'grp_1'=8,'node_0'=4,'node_1'=2] {'node_0','node_1'}, dimensions={0} | all-to-all | bytes 196608 | tf_op jit(solution)/shard_map/all_to_all | solution.py:172
  79.2 16.8 %all_to_all.21 = f32[32,24,128]{2,1,0:T(8,128)S(1)} all-to-all(f32[32,24,128]{2,1,0:T(8,128)S(1)} %broadcast_in_dim.15), channel_id=1, replica_groups=mesh['grp_0'=4,'grp_1'=8,'node_0'=4,'node_1'=2] {'grp_0','grp_1'}, dimensions={0} | all-to-all | bytes 786432 | tf_op jit(solution)/shard_map/all_to_all | solution.py:166
  96.0 0.6 broadcast_in_dim.16
  96.6 7.4 %all-to-all-start.3 = ((f32[8,24,128]{2,1,0:T(8,128)}), f32[8,24,128]{2,1,0:T(8,128)S(1)}, u32[]{:S(2)}, u32[]{:S(2)}) async-start(f32[8,24,128]{2,1,0:T(8,128)} %broadcast_in_dim.16), calls=%async_computation.3 | async-start | bytes 196608 | tf_op jit(solution)/shard_map/all_to_all | solution.py:166
  104.0 0.9 copy.12
  104.9 4.1 %all-to-all-done.3 = f32[8,24,128]{2,1,0:T(8,128)S(1)} async-done(((f32[8,24,128]{2,1,0:T(8,128)}), f32[8,24,128]{2,1,0:T(8,128)S(1)}, u32[]{:S(2)}, u32[]{:S(2)}) %all-to-all-start.3) | async-done | bytes 98336 | tf_op jit(solution)/shard_map/all_to_all | solution.py:166
  109.0 0.6 copy.13
  (5 shorter events, 0.1 us)
Async XLA Ops:
  5.9 55.1 %all-to-all-start = ((bf16[32,7,32,128]{3,2,1,0:T(8,128)(2,1)}), bf16[32,7,32,128]{3,2,1,0:T(8,128)(2,1)S(1)}, u32[]{:S(2)}, u32[]{:S(2)}) async-start(bf16[32,7,32,128]{3,2,1,0:T(8,128)(2,1)} %pack.1), calls=%async_computation | async-start | bytes 3670016 | tf_op jit(solution)/shard_map/all_to_all | solution.py:229
  96.6 12.4 %all-to-all-start.3 = ((f32[8,24,128]{2,1,0:T(8,128)}), f32[8,24,128]{2,1,0:T(8,128)S(1)}, u32[]{:S(2)}, u32[]{:S(2)}) async-start(f32[8,24,128]{2,1,0:T(8,128)} %broadcast_in_dim.16), calls=%async_computation.3 | async-start | bytes 196608 | tf_op jit(solution)/shard_map/all_to_all | solution.py:166

commit v4 on v3

--- a/solution.py
+++ b/solution.py
@@ -10,9 +10,11 @@
 
 STEPS = 6
 TIMES = STEPS + 1
-GRP = ("grp_0", "grp_1")
+GRP = ("grp_0", "grp_1", "grp_2")
 NODE = ("node_0", "node_1")
-GRP_NODE = ("grp_0", "grp_1", "node_0", "node_1")
+GRP_NODE = GRP + NODE
+SPREAD = ("grp_1", "node_0", "node_1")
+REST = ("grp_0", "grp_2")
 
 DT = 0.5
 MIB = 1 << 20
@@ -91,31 +93,40 @@
     )
 
 
+def hold_kernel(after, weights, held, sem):
+    load = pltpu.make_async_copy(
+        weights.at[pl.ds(0, held.shape[0]), :, pl.ds(0, held.shape[2])], held, sem
+    )
+    load.start()
+    load.wait()
+
+
 def evolve_kernel(
-    own, parcel, weights, initial, noise, lead, state, sensors,
-    stack, start, rate, gains, left, coupled, potential, sems, *, tiles, piece, width, ahead
+    own, parcel, held, weights, initial, noise, lead, state, sensors,
+    stack, start, rate, gains, left, coupled, potential, sems, out_sems, *, tiles, piece, width
 ):
     replicas, nodes = noise.shape
     chunks = nodes // width
+    early = held.shape[0]
     loads = [
-        pltpu.make_async_copy(weights.at[:, :, pl.ds(i * width, width)], stack.at[i], sems.at[i])
+        pltpu.make_async_copy(
+            weights.at[pl.ds(first, tiles - first), :, pl.ds(i * width, width)],
+            stack.at[i, pl.ds(first, tiles - first)],
+            sems.at[i],
+        )
         for i in range(chunks)
+        for first in [0 if i else early]
     ]
     others = [
         pltpu.make_async_copy(initial, start, sems.at[chunks]),
         pltpu.make_async_copy(noise, rate, sems.at[chunks + 1]),
         pltpu.make_async_copy(lead, gains, sems.at[chunks + 2]),
     ]
-    loads[0].start()
-    for other in others:
-        other.start()
-    for load in loads[1:ahead]:
+    for load in (loads[0], *others, *loads[1:]):
         load.start()
     fill_left(own, parcel, left, tiles, piece)
-    lane = width
-
-    def strip(i, carry):
-        lanes = pl.ds(pl.multiple_of(i * lane, lane), lane)
+
+    def strip(lanes):
         y = [start[r, :, lanes] for r in range(3)]
         z = [DT * start[r, :, lanes] for r in range(3, 6)]
         noisy = DRIVE * rate[:, lanes] + G1
@@ -139,26 +150,43 @@
                     + (0.5 * DRIVE) * coupled[(s + 2) * replicas : (s + 3) * replicas, lanes]
                 )
         for r in range(3):
-            state[r, :, lanes] = y[r]
-            state[r + 3, :, lanes] = (1.0 / DT) * z[r]
-        return carry
-
-    for i in range(chunks):
-        loads[i].wait()
-        if i + ahead < chunks:
-            loads[i + ahead].start()
-        coupled[:, i * width : (i + 1) * width] = jnp.dot(
-            left[...],
-            stack[i].reshape(tiles * piece, width),
+            start[r, :, lanes] = y[r]
+            start[r + 3, :, lanes] = (1.0 / DT) * z[r]
+
+    stores = []
+    def product(first, some):
+        depth = some.shape[0] * piece
+        return jnp.dot(
+            left[:, first * piece : first * piece + depth],
+            some.reshape(depth, width),
             preferred_element_type=jnp.float32,
         )
+
+    for i in range(chunks):
+        lanes = slice(i * width, (i + 1) * width)
+        if i:
+            loads[i].wait()
+            coupled[:, lanes] = product(0, stack[i])
+        else:
+            coupled[:, lanes] = product(0, held[...])
+            loads[i].wait()
+            coupled[:, lanes] = coupled[:, lanes] + product(early, stack[i, early:])
         if i == 0:
             for other in others:
                 other.wait()
-        lax.fori_loop(i * width // lane, (i + 1) * width // lane, strip, 0)
-    sensors[...] = lax.dot_general(
+        strip(lanes)
+        stores.append(
+            pltpu.make_async_copy(
+                start.at[:, :, lanes], state.at[:, :, lanes], out_sems.at[i]
+            )
+        )
+        stores[-1].start()
+    local = lax.dot_general(
         potential[...], gains[...], (((1,), (1,)), ((), ())), preferred_element_type=jnp.float32
     )
+    sensors[...] = local.reshape(sensors.shape)
+    for store in stores:
+        store.wait()
 
 
 def to_all(x, axis):
@@ -166,12 +194,10 @@
     return lax.all_to_all(copies, axis, split_axis=0, concat_axis=0, tiled=True)
 
 
-def total_of(x):
-    columns = lax.axis_size(NODE)
-    parts = x.reshape(columns, -1, x.shape[-1])
-    mine = jnp.sum(lax.all_to_all(parts, NODE, split_axis=0, concat_axis=0, tiled=True), axis=0)
-    mine = jnp.sum(to_all(mine, GRP), axis=0)
-    return to_all(mine, NODE).reshape(x.shape)
+def total_of(parts):
+    mine = jnp.sum(lax.all_to_all(parts, SPREAD, split_axis=0, concat_axis=0, tiled=True), axis=0)
+    mine = jnp.sum(to_all(mine, REST), axis=0)
+    return to_all(mine, SPREAD)
 
 
 def body(
@@ -229,28 +255,48 @@
     parcel = lax.all_to_all(packed, GRP, split_axis=0, concat_axis=0, tiled=True)
 
     tile_stack = outside(weights.reshape(tiles, piece, nodes))
-    width = 512
+    width, early = nodes // 2, tiles // 2
+    spread = lax.axis_size(SPREAD)
+    chunks = nodes // width
+    held = pl.pallas_call(
+        hold_kernel,
+        out_shape=pltpu.VMEM((early, piece, width), bf16),
+        in_specs=[far, far],
+        out_specs=vmem,
+        scratch_shapes=[pltpu.SemaphoreType.DMA],
+        compiler_params=pltpu.CompilerParams(vmem_limit_bytes=4 * MIB),
+        name="hold",
+    )(outside(packed), tile_stack)
     state, local = pl.pallas_call(
-        functools.partial(evolve_kernel, tiles=tiles, piece=piece, width=width, ahead=2),
+        functools.partial(evolve_kernel, tiles=tiles, piece=piece, width=width),
         out_shape=(
-            pltpu.VMEM(initial.shape, f32),
-            pltpu.VMEM((STEPS * replicas, sensors_count), f32),
+            pltpu.HBM(initial.shape, f32),
+            pltpu.VMEM((spread, STEPS * replicas // spread, sensors_count), f32),
         ),
-        in_specs=[smem, vmem, far, far, far, far],
-        out_specs=(vmem, vmem),
+        in_specs=[smem, vmem, vmem, far, far, far, far],
+        out_specs=(far, vmem),
         scratch_shapes=[
-            pltpu.VMEM((nodes // width, tiles, piece, width), bf16),
+            pltpu.VMEM((chunks, tiles, piece, width), bf16),
             pltpu.VMEM(initial.shape, f32),
             pltpu.VMEM(afferent_noise_level.shape, f32),
             pltpu.VMEM(lead_field.shape, bf16),
             pltpu.VMEM((TIMES * replicas, tiles * piece), bf16),
             pltpu.VMEM((TIMES * replicas, nodes), f32),
             pltpu.VMEM((STEPS * replicas, nodes), bf16),
-            pltpu.SemaphoreType.DMA((nodes // width + 3,)),
+            pltpu.SemaphoreType.DMA((chunks + 3,)),
+            pltpu.SemaphoreType.DMA((chunks,)),
         ],
-        compiler_params=pltpu.CompilerParams(vmem_limit_bytes=24 * MIB),
+        compiler_params=pltpu.CompilerParams(vmem_limit_bytes=32 * MIB),
         name="evolve",
-    )(own, near(parcel), tile_stack, outside(initial), outside(afferent_noise_level), outside(lead_field))
+    )(
+        own,
+        near(parcel),
+        near(held),
+        tile_stack,
+        outside(initial),
+        outside(afferent_noise_level),
+        outside(lead_field),
+    )
 
     total = total_of(local)
     sensors = jnp.transpose(total.reshape(STEPS, replicas, sensors_count), (0, 2, 1))
@@ -258,7 +304,7 @@
 
 
 def solution(mesh):
-    finer = Mesh(mesh.devices.reshape(4, 8, 4, 2), GRP_NODE)
+    finer = Mesh(mesh.devices.reshape(2, 2, 8, 4, 2), GRP_NODE)
     placed = (
         P(None, None, GRP_NODE),
         P(None, GRP_NODE),

time: 110 us -> 107 us (0.973)
  blocking collectives: 28.6 us -> 37.9 us
  starting transfers between devices: 19.4 us -> 11.8 us
  waiting for transfers between devices: 47.1 us -> 41.6 us
  Pallas kernels: 10.6 us -> 12.8 us
  local copies, waits for them, and re-layouts: 2.2 us -> 0.68 us
    all_to_all x1 -> x2, blocking collectives: 16.8 us -> 25 us  [to_all(): return lax.all_to_all(copies, axis, split_axis=0, concat_axis=0, tiled=True)]
    all_to_all x1 -> x0, starting transfers between devices: 7.37 us -> none  [to_all(): return lax.all_to_all(copies, axis, split_axis=0, concat_axis=0, tiled=True)]
    all_to_all x1 -> x0, waiting for transfers between devices: 4.12 us -> none  [to_all(): return lax.all_to_all(copies, axis, split_axis=0, concat_axis=0, tiled=True)]
    unnamed x2 -> x0, local copies, waits for them, and re-layouts: 1.52 us -> none
    pallas_call x0 -> x1, Pallas kernels: none -> 1.42 us  [body(): pl.pallas_call(hold_kernel, out_shape=pltpu.VMEM((early, piece, width), b...]
    all_to_all x1, waiting for transfers between devices: 43 us -> 41.6 us  [body(): lax.all_to_all(packed, GRP, split_axis=0, concat_axis=0, tiled=True)]
    all_to_all x1, blocking collectives: 11.8 us -> 13 us  [total_of(): lax.all_to_all(parts, SPREAD, split_axis=0, concat_axis=0, tiled=True)]
  transfers between devices with their start and end apart: 2 -> 1, of which waited for: 2 -> 1; matrix products, arithmetic and copies ran while one was open for 1% -> 0% of each run, Pallas kernels for 0% -> 1%
where the time goes in v4:
time: 107 us
  waiting for transfers between devices  41.6 us (39%)
  blocking collectives  37.9 us (35%)
  Pallas kernels  12.8 us (12%)
  starting transfers between devices  11.8 us (11%)
    all_to_all x1, waiting for transfers between devices, body(): lax.all_to_all(packed, GRP, split_axis=0, concat_axis=0, tiled=True)  41.6 us
    all_to_all x2, blocking collectives, to_all(): return lax.all_to_all(copies, axis, split_axis=0, concat_axis=0, tiled=True)  25 us
    all_to_all x1, blocking collectives, total_of(): lax.all_to_all(parts, SPREAD, split_axis=0, concat_axis=0, tiled=True)  13 us
    all_to_all x1, starting transfers between devices, body(): lax.all_to_all(packed, GRP, split_axis=0, concat_axis=0, tiled=True)  11.8 us
    pallas_call x1, Pallas kernels, body(): pl.pallas_call(functools.partial(evolve_kernel, tiles=tiles, piece=piece,...  6.77 us
    pallas_call x1, Pallas kernels, body(): pl.pallas_call(functools.partial(pack_kernel, owners=owners, columns=colu...  4.59 us
  transfers between devices with their start and end apart: 1, of which 1 were waited for; matrix products, arithmetic and copies ran while one was open for 0% of the time, Pallas kernels for 1%

profile of v4, /device:TPU:1, one launch (start us, length us, event | category | flops | bytes accessed | tf_op | source)
XLA Modules:
  0.0 106.5 jit_solution(13467440300758081422)
XLA Ops:
  0.7 0.9 fusion
  1.6 4.6 %pack.1.after = bf16[32,7,32,128]{3,2,1,0:T(8,128)(2,1)} custom-call(s32[256]{0:T(256)S(1)} %get-tuple-element.6.codes, s32[1]{0:T(128)} %bitcast.3.column, bf16[64,32,1024]{2,1,0:T(8,128)(2,1)} %history.1, f32[6,32,1024]{2,1,0:T(8,128)} %initial.3), custom_call_target="tpu_custom_call" | custom-call | tf_op jit(solution)/shard_map/pack/pallas_call | solution.py:237
  6.2 11.8 %all-to-all-start = ((bf16[32,7,32,128]{3,2,1,0:T(8,128)(2,1)}), bf16[32,7,32,128]{3,2,1,0:T(8,128)(2,1)S(1)}, u32[]{:S(2)}, u32[]{:S(2)}) async-start(bf16[32,7,32,128]{3,2,1,0:T(8,128)(2,1)} %pack.1.after), calls=%async_computation | async-start | bytes 3670016 | tf_op jit(solution)/shard_map/all_to_all | solution.py:255
  18.0 1.4 %hold.1.held = bf16[12,128,512]{2,1,0:T(8,128)(2,1)S(1)} custom-call(bf16[32,7,32,128]{3,2,1,0:T(8,128)(2,1)} %pack.1.after, bf16[24,128,1024]{2,1,0:T(8,128)(2,1)} %bitcast.13), custom_call_target="tpu_custom_call" | custom-call | tf_op jit(solution)/shard_map/hold/pallas_call | solution.py:261
  19.4 41.6 %all-to-all-done.parcel = bf16[32,7,32,128]{3,2,1,0:T(8,128)(2,1)S(1)} async-done(((bf16[32,7,32,128]{3,2,1,0:T(8,128)(2,1)}), bf16[32,7,32,128]{3,2,1,0:T(8,128)(2,1)S(1)}, u32[]{:S(2)}, u32[]{:S(2)}) %all-to-all-start) | async-done | bytes 1835040 | tf_op jit(solution)/shard_map/all_to_all | solution.py:255
  61.1 6.8 %evolve.1 = (f32[6,32,1024]{2,1,0:T(8,128)}, f32[16,12,128]{2,1,0:T(8,128)S(1)}) custom-call(s32[24]{0:T(128)S(1)} %broadcast_add_fusion.own, bf16[32,7,32,128]{3,2,1,0:T(8,128)(2,1)S(1)} %all-to-all-done.parcel, bf16[12,128,512]{2,1,0:T(8,128)(2,1)S(1)} %hold.1.held, bf16[24,128,1024]{2,1,0:T(8,128)(2,1)} %bitcast.14, f32[6,32,1024]{2,1,0:T(8,128)} %initial.3, ...), custom_call_target="tpu_custom_call" | custom-call | tf_op jit(solution)/shard_map/evolve/pallas_call | solution.py:270
  67.9 13.0 %all_to_all.20 = f32[16,12,128]{2,1,0:T(8,128)S(1)} all-to-all(f32[16,12,128]{2,1,0:T(8,128)S(1)} %get-tuple-element.5), channel_id=1, replica_groups=mesh['grp_0'=2,'grp_1'=2,'grp_2'=8,'node_0'=4,'node_1'=2] {'grp_1','node..., dimensions={0} | all-to-all | bytes 196608 | tf_op jit(solution)/shard_map/all_to_all | solution.py:198
  80.9 14.3 %all_to_all.21 = f32[16,12,128]{2,1,0:T(8,128)S(1)} all-to-all(f32[16,12,128]{2,1,0:T(8,128)S(1)} %broadcast_in_dim.15), channel_id=1, replica_groups=mesh['grp_0'=2,'grp_1'=2,'grp_2'=8,'node_0'=4,'node_1'=2] {'grp_0','grp_2'}, dimensions={0} | all-to-all | bytes 196608 | tf_op jit(solution)/shard_map/all_to_all | solution.py:194
  95.2 10.7 %all_to_all.22 = f32[16,12,128]{2,1,0:T(8,128)S(1)} all-to-all(f32[16,12,128]{2,1,0:T(8,128)S(1)} %broadcast_in_dim.16), channel_id=1, replica_groups=mesh['grp_0'=2,'grp_1'=2,'grp_2'=8,'node_0'=4,'node_1'=2] {'grp_1','node..., dimensions={0} | all-to-all | bytes 196608 | tf_op jit(solution)/shard_map/all_to_all | solution.py:194
  105.9 0.6 reshape.20
  (6 shorter events, 0.1 us)
Async XLA Ops:
  6.2 54.9 %all-to-all-start = ((bf16[32,7,32,128]{3,2,1,0:T(8,128)(2,1)}), bf16[32,7,32,128]{3,2,1,0:T(8,128)(2,1)S(1)}, u32[]{:S(2)}, u32[]{:S(2)}) async-start(bf16[32,7,32,128]{3,2,1,0:T(8,128)(2,1)} %pack.1.after), calls=%async_computation | async-start | bytes 3670016 | tf_op jit(solution)/shard_map/all_to_all | solution.py:255

commit v5 on v4

--- a/solution.py
+++ b/solution.py
@@ -25,42 +25,47 @@
 
 
 def pack_kernel(
-    codes, column, history, initial, out, parts, rows, fire, gets, puts, row_sem, *, owners, columns, piece, cycle
+    group, column, groups, subs, delays, counts, history, initial, out,
+    whole, parts, rows, tables, limits, codes, chosen, gets, puts, row_sem, table_sems, code_sem, *, columns, piece
 ):
-    replicas = fire.shape[0]
-    load = pltpu.make_async_copy(initial.at[pl.ds(1, 2)], rows, row_sem)
-    load.start()
-
-    def code_of(g):
-        return codes[g * columns + column[0]]
-
-    def get(g):
-        start = jnp.minimum((code_of(g) >> 3), cycle - TIMES)
-        sub = (code_of(g) & 7) * piece
-        return pltpu.make_async_copy(
-            history.at[pl.ds(start, TIMES), :, pl.ds(sub, piece)], parts.at[g], gets.at[g]
+    owners = out.shape[0]
+    tiles, blocks = tables.shape[1:]
+    cycle = history.shape[0]
+    some = cycle // gets.shape[0]
+    loads = [
+        pltpu.make_async_copy(
+            history.at[pl.ds(i * some, some)], whole.at[pl.ds(i * some, some)], gets.at[i]
         )
+        for i in range(gets.shape[0])
+    ]
+    load_rows = pltpu.make_async_copy(initial.at[pl.ds(1, 2)], rows, row_sem)
+    lookups = [
+        pltpu.make_async_copy(table, tables.at[i], table_sems.at[i])
+        for i, table in enumerate((groups, subs, delays))
+    ] + [pltpu.make_async_copy(counts, limits, table_sems.at[3])]
+    for load in (*lookups, load_rows, *loads):
+        load.start()
+    for load in lookups:
+        load.wait()
+    lanes = lax.broadcasted_iota(jnp.int32, (tiles, blocks), 0)
+    mine = (tables[0] == group[0]) & (lanes < limits[...])
+    code = jnp.sum(jnp.where(mine, (cycle - tables[2]) * 8 + tables[1], 0), axis=0, keepdims=True)
+    codes[...] = code
+    move = pltpu.make_async_copy(codes, chosen, code_sem)
+    move.start()
+    load_rows.wait()
+    whole[cycle] = firing(rows[0] - rows[1]).astype(whole.dtype)
+    move.wait()
+    for load in loads:
+        load.wait()
 
     def put(g):
         return pltpu.make_async_copy(parts.at[g], out.at[g], puts.at[g])
 
-    def reaches(g):
-        return (code_of(g) >> 3) + TIMES > cycle
-
     for g in range(owners):
-        get(g).start()
-    load.wait()
-    fire[...] = firing(rows[0] - rows[1]).astype(fire.dtype)
-    for g in range(owners):
-        get(g).wait()
-
-        @pl.when(reaches(g))
-        def _():
-            sub = pl.multiple_of((code_of(g) & 7) * piece, piece)
-            for t in range(TIMES - 1):
-                parts[g, t] = parts[g, t + 1]
-            parts[g, TIMES - 1] = fire[:, pl.ds(sub, piece)]
-
+        code = chosen[0, g * columns + column[0]]
+        sub = pl.multiple_of((code & 7) * piece, piece)
+        parts[g] = whole[pl.ds(code >> 3, TIMES), :, pl.ds(sub, piece)]
         put(g).start()
     for g in range(owners):
         put(g).wait()
@@ -168,9 +173,9 @@
             loads[i].wait()
             coupled[:, lanes] = product(0, stack[i])
         else:
-            coupled[:, lanes] = product(0, held[...])
+            part = product(0, held[...])
             loads[i].wait()
-            coupled[:, lanes] = coupled[:, lanes] + product(early, stack[i, early:])
+            coupled[:, lanes] = part + product(early, stack[i, early:])
         if i == 0:
             for other in others:
                 other.wait()
@@ -213,12 +218,10 @@
     sensors_count = lead_field.shape[0]
     lanes = jnp.arange(tiles, dtype=jnp.int32)
 
-    group_t, sub_t, delay_t = src_group.T, src_sub.T, delays.T
+    group_t = src_group.T
+    group = my_group.astype(jnp.int32).reshape(1)
+    column = my_column.astype(jnp.int32).reshape(1)
     live = lanes[:, None] < counts[None, :]
-    codes = jnp.sum(
-        jnp.where((group_t == my_group) & live, (cycle - delay_t) * 8 + sub_t, 0), axis=0
-    )
-    column = my_column.astype(jnp.int32).reshape(1)
     mine = (jnp.arange(counts.shape[0], dtype=jnp.int32) == myself)[None, :] & live
     own = jnp.sum(jnp.where(mine, group_t + 1, 0), axis=1) - 1
 
@@ -235,23 +238,36 @@
 
 
     packed = pl.pallas_call(
-        functools.partial(
-            pack_kernel, owners=owners, columns=columns, piece=piece, cycle=cycle
-        ),
+        functools.partial(pack_kernel, columns=columns, piece=piece),
         out_shape=pltpu.HBM((owners, TIMES, replicas, piece), bf16),
-        in_specs=[smem, smem, far, far],
+        in_specs=[smem, smem, far, far, far, far, far, far],
         out_specs=far,
         scratch_shapes=[
+            pltpu.VMEM((cycle + 1, replicas, nodes), bf16),
             pltpu.VMEM((owners, TIMES, replicas, piece), bf16),
             pltpu.VMEM((2, replicas, nodes), f32),
-            pltpu.VMEM((replicas, nodes), bf16),
-            pltpu.SemaphoreType.DMA((owners,)),
+            pltpu.VMEM((3, *group_t.shape), jnp.int32),
+            pltpu.VMEM((1, counts.shape[0]), jnp.int32),
+            pltpu.VMEM((1, counts.shape[0]), jnp.int32),
+            pltpu.SMEM((1, counts.shape[0]), jnp.int32),
+            pltpu.SemaphoreType.DMA((4,)),
             pltpu.SemaphoreType.DMA((owners,)),
             pltpu.SemaphoreType.DMA,
+            pltpu.SemaphoreType.DMA((4,)),
+            pltpu.SemaphoreType.DMA,
         ],
-        compiler_params=pltpu.CompilerParams(vmem_limit_bytes=8 * MIB),
+        compiler_params=pltpu.CompilerParams(vmem_limit_bytes=16 * MIB),
         name="pack",
-    )(codes, column, outside(history), outside(initial))
+    )(
+        group,
+        column,
+        outside(group_t),
+        outside(src_sub.T),
+        outside(delays.T),
+        outside(counts[None, :]),
+        outside(history),
+        outside(initial),
+    )
     parcel = lax.all_to_all(packed, GRP, split_axis=0, concat_axis=0, tiled=True)
 
     tile_stack = outside(weights.reshape(tiles, piece, nodes))

time: 107 us -> 105 us (0.981)
  no operation moved by 1% of the time
where the time goes in v5:
time: 105 us
  waiting for transfers between devices  41.8 us (40%)
  blocking collectives  37.6 us (36%)
  Pallas kernels  11.9 us (11%)
  starting transfers between devices  11.9 us (11%)
    all_to_all x1, waiting for transfers between devices, body(): lax.all_to_all(packed, GRP, split_axis=0, concat_axis=0, tiled=True)  41.8 us
    all_to_all x2, blocking collectives, to_all(): return lax.all_to_all(copies, axis, split_axis=0, concat_axis=0, tiled=True)  25 us
    all_to_all x1, blocking collectives, total_of(): lax.all_to_all(parts, SPREAD, split_axis=0, concat_axis=0, tiled=True)  12.6 us
    all_to_all x1, starting transfers between devices, body(): lax.all_to_all(packed, GRP, split_axis=0, concat_axis=0, tiled=True)  11.9 us
    pallas_call x1, Pallas kernels, body(): pl.pallas_call(functools.partial(evolve_kernel, tiles=tiles, piece=piece,...  6.5 us
    pallas_call x1, Pallas kernels, body(): pl.pallas_call(functools.partial(pack_kernel, columns=columns, piece=piec...  3.96 us
  transfers between devices with their start and end apart: 1, of which 1 were waited for; matrix products, arithmetic and copies ran while one was open for 0% of the time, Pallas kernels for 1%

profile of v5, /device:TPU:1, one launch (start us, length us, event | category | flops | bytes accessed | tf_op | source)
XLA Modules:
  0.0 104.7 jit_solution(4803515075223039720)
XLA Ops:
  0.6 4.0 %pack.1.after = bf16[32,7,32,128]{3,2,1,0:T(8,128)(2,1)} custom-call(s32[1]{0:T(128)} %bitcast.1.group, s32[1]{0:T(128)} %bitcast.2.column, s32[24,256]{1,0:T(8,128)} %bitcast.11, s32[24,256]{1,0:T(8,128)} %bitcast.13, s32[24,256]{1,0:T(8,128)} %bitcast.14, s32[1,256]{1,0:T(1,128)} %bitcast.15, bf16[64,32,1024]{2,1,0:T(8,128)(2,1)} %history.1, ...), custom_call_target="tpu_custom_call" | custom-call | tf_op jit(solution)/shard_map/pack/pallas_call | solution.py:240
  4.6 11.9 %all-to-all-start = ((bf16[32,7,32,128]{3,2,1,0:T(8,128)(2,1)}), bf16[32,7,32,128]{3,2,1,0:T(8,128)(2,1)S(1)}, u32[]{:S(2)}, u32[]{:S(2)}) async-start(bf16[32,7,32,128]{3,2,1,0:T(8,128)(2,1)} %pack.1.after), calls=%async_computation | async-start | bytes 3670016 | tf_op jit(solution)/shard_map/all_to_all | solution.py:271
  16.5 0.0 copy-start
  16.5 0.0 copy-start.1
  16.5 1.4 %hold.1.held = bf16[12,128,512]{2,1,0:T(8,128)(2,1)S(1)} custom-call(bf16[32,7,32,128]{3,2,1,0:T(8,128)(2,1)} %pack.1.after, bf16[24,128,1024]{2,1,0:T(8,128)(2,1)} %bitcast.9), custom_call_target="tpu_custom_call" | custom-call | tf_op jit(solution)/shard_map/hold/pallas_call | solution.py:277
  18.0 0.0 copy-done
  18.0 0.0 copy-done.1
  18.0 0.1 select_reduce_fusion
  18.1 41.8 %all-to-all-done.parcel = bf16[32,7,32,128]{3,2,1,0:T(8,128)(2,1)S(1)} async-done(((bf16[32,7,32,128]{3,2,1,0:T(8,128)(2,1)}), bf16[32,7,32,128]{3,2,1,0:T(8,128)(2,1)S(1)}, u32[]{:S(2)}, u32[]{:S(2)}) %all-to-all-start) | async-done | bytes 1835040 | tf_op jit(solution)/shard_map/all_to_all | solution.py:271
  59.9 6.5 %evolve.1 = (f32[6,32,1024]{2,1,0:T(8,128)}, f32[16,12,128]{2,1,0:T(8,128)S(1)}) custom-call(s32[24]{0:T(128)S(1)} %broadcast_add_fusion.own, bf16[32,7,32,128]{3,2,1,0:T(8,128)(2,1)S(1)} %all-to-all-done.parcel, bf16[12,128,512]{2,1,0:T(8,128)(2,1)S(1)} %hold.1.held, bf16[24,128,1024]{2,1,0:T(8,128)(2,1)} %bitcast.10, f32[6,32,1024]{2,1,0:T(8,128)} %initial.3, ...), custom_call_target="tpu_custom_call" | custom-call | tf_op jit(solution)/shard_map/evolve/pallas_call | solution.py:286
  66.4 12.6 %all_to_all.20 = f32[16,12,128]{2,1,0:T(8,128)S(1)} all-to-all(f32[16,12,128]{2,1,0:T(8,128)S(1)} %get-tuple-element.5), channel_id=1, replica_groups=mesh['grp_0'=2,'grp_1'=2,'grp_2'=8,'node_0'=4,'node_1'=2] {'grp_1','node..., dimensions={0} | all-to-all | bytes 196608 | tf_op jit(solution)/shard_map/all_to_all | solution.py:203
  79.1 14.3 %all_to_all.21 = f32[16,12,128]{2,1,0:T(8,128)S(1)} all-to-all(f32[16,12,128]{2,1,0:T(8,128)S(1)} %broadcast_in_dim.18), channel_id=1, replica_groups=mesh['grp_0'=2,'grp_1'=2,'grp_2'=8,'node_0'=4,'node_1'=2] {'grp_0','grp_2'}, dimensions={0} | all-to-all | bytes 196608 | tf_op jit(solution)/shard_map/all_to_all | solution.py:199
  93.4 10.7 %all_to_all.22 = f32[16,12,128]{2,1,0:T(8,128)S(1)} all-to-all(f32[16,12,128]{2,1,0:T(8,128)S(1)} %broadcast_in_dim.19), channel_id=1, replica_groups=mesh['grp_0'=2,'grp_1'=2,'grp_2'=8,'node_0'=4,'node_1'=2] {'grp_1','node..., dimensions={0} | all-to-all | bytes 196608 | tf_op jit(solution)/shard_map/all_to_all | solution.py:199
  104.1 0.6 reshape.24
  (6 shorter events, 0.1 us)
Async XLA Ops:
  4.6 55.3 %all-to-all-start = ((bf16[32,7,32,128]{3,2,1,0:T(8,128)(2,1)}), bf16[32,7,32,128]{3,2,1,0:T(8,128)(2,1)S(1)}, u32[]{:S(2)}, u32[]{:S(2)}) async-start(bf16[32,7,32,128]{3,2,1,0:T(8,128)(2,1)} %pack.1.after), calls=%async_computation | async-start | bytes 3670016 | tf_op jit(solution)/shard_map/all_to_all | solution.py:271
  16.5 1.5 %copy-start = (s32[256,24]{0,1:T(8,128)S(1)}, s32[256,24]{0,1:T(8,128)}, u32[]{:S(2)}) copy-start(s32[256,24]{0,1:T(8,128)} %param.14) | copy-start | bytes 73732
  16.5 1.5 %copy-start.1 = (s32[256]{0:T(256)S(1)}, s32[256]{0:T(256)}, u32[]{:S(2)}) copy-start(s32[256]{0:T(256)} %param.17) | copy-start | bytes 3076

commit v6 on v5

--- a/solution.py
+++ b/solution.py
@@ -189,7 +189,10 @@
     local = lax.dot_general(
         potential[...], gains[...], (((1,), (1,)), ((), ())), preferred_element_type=jnp.float32
     )
-    sensors[...] = local.reshape(sensors.shape)
+    for i in range(sensors.shape[0]):
+        for j in range(sensors.shape[1]):
+            row = (i * sensors.shape[1] + j) * 4
+            sensors[i, j] = local[row : row + 4]
     for store in stores:
         store.wait()
 
@@ -287,7 +290,7 @@
         functools.partial(evolve_kernel, tiles=tiles, piece=piece, width=width),
         out_shape=(
             pltpu.HBM(initial.shape, f32),
-            pltpu.VMEM((spread, STEPS * replicas // spread, sensors_count), f32),
+            pltpu.VMEM((spread, STEPS * replicas // spread // 4, 4, sensors_count), f32),
         ),
         in_specs=[smem, vmem, vmem, far, far, far, far],
         out_specs=(far, vmem),

time: 105 us -> 104 us (level)
  no operation moved by 1% of the time
where the time goes in v6:
time: 104 us
  waiting for transfers between devices  41.8 us (40%)
  blocking collectives  36.9 us (35%)
  Pallas kernels  11.9 us (11%)
  starting transfers between devices  11.9 us (11%)
    all_to_all x1, waiting for transfers between devices, body(): lax.all_to_all(packed, GRP, split_axis=0, concat_axis=0, tiled=True)  41.8 us
    all_to_all x2, blocking collectives, to_all(): return lax.all_to_all(copies, axis, split_axis=0, concat_axis=0, tiled=True)  24.6 us
    all_to_all x1, blocking collectives, total_of(): lax.all_to_all(parts, SPREAD, split_axis=0, concat_axis=0, tiled=True)  12.3 us
    all_to_all x1, starting transfers between devices, body(): lax.all_to_all(packed, GRP, split_axis=0, concat_axis=0, tiled=True)  11.9 us
    pallas_call x1, Pallas kernels, body(): pl.pallas_call(functools.partial(evolve_kernel, tiles=tiles, piece=piece,...  6.5 us
    pallas_call x1, Pallas kernels, body(): pl.pallas_call(functools.partial(pack_kernel, columns=columns, piece=piec...  3.96 us
  transfers between devices with their start and end apart: 1, of which 1 were waited for; matrix products, arithmetic and copies ran while one was open for 0% of the time, Pallas kernels for 1%

profile of v6, /device:TPU:1, one launch (start us, length us, event | category | flops | bytes accessed | tf_op | source)
XLA Modules:
  0.0 104.1 jit_solution(12985180287572184244)
XLA Ops:
  0.6 4.0 %pack.1.after = bf16[32,7,32,128]{3,2,1,0:T(8,128)(2,1)} custom-call(s32[1]{0:T(128)} %bitcast.1.group, s32[1]{0:T(128)} %bitcast.2.column, s32[24,256]{1,0:T(8,128)} %bitcast.14, s32[24,256]{1,0:T(8,128)} %bitcast.15, s32[24,256]{1,0:T(8,128)} %bitcast.16, s32[1,256]{1,0:T(1,128)} %bitcast.17, bf16[64,32,1024]{2,1,0:T(8,128)(2,1)} %history.1, ...), custom_call_target="tpu_custom_call" | custom-call | tf_op jit(solution)/shard_map/pack/pallas_call | solution.py:243
  4.6 11.9 %all-to-all-start = ((bf16[32,7,32,128]{3,2,1,0:T(8,128)(2,1)}), bf16[32,7,32,128]{3,2,1,0:T(8,128)(2,1)S(1)}, u32[]{:S(2)}, u32[]{:S(2)}) async-start(bf16[32,7,32,128]{3,2,1,0:T(8,128)(2,1)} %pack.1.after), calls=%async_computation | async-start | bytes 3670016 | tf_op jit(solution)/shard_map/all_to_all | solution.py:274
  16.5 0.0 copy-start
  16.5 0.0 copy-start.1
  16.5 1.4 %hold.1.held = bf16[12,128,512]{2,1,0:T(8,128)(2,1)S(1)} custom-call(bf16[32,7,32,128]{3,2,1,0:T(8,128)(2,1)} %pack.1.after, bf16[24,128,1024]{2,1,0:T(8,128)(2,1)} %bitcast.11), custom_call_target="tpu_custom_call" | custom-call | tf_op jit(solution)/shard_map/hold/pallas_call | solution.py:280
  18.0 0.0 copy-done
  18.0 0.0 copy-done.1
  18.0 0.1 select_reduce_fusion
  18.1 41.8 %all-to-all-done.parcel = bf16[32,7,32,128]{3,2,1,0:T(8,128)(2,1)S(1)} async-done(((bf16[32,7,32,128]{3,2,1,0:T(8,128)(2,1)}), bf16[32,7,32,128]{3,2,1,0:T(8,128)(2,1)S(1)}, u32[]{:S(2)}, u32[]{:S(2)}) %all-to-all-start) | async-done | bytes 1835040 | tf_op jit(solution)/shard_map/all_to_all | solution.py:274
  59.9 6.5 %evolve.1 = (f32[6,32,1024]{2,1,0:T(8,128)}, f32[16,3,4,128]{3,2,1,0:T(4,128)S(1)}) custom-call(s32[24]{0:T(128)S(1)} %broadcast_add_fusion.own, bf16[32,7,32,128]{3,2,1,0:T(8,128)(2,1)S(1)} %all-to-all-done.parcel, bf16[12,128,512]{2,1,0:T(8,128)(2,1)S(1)} %hold.1.held, bf16[24,128,1024]{2,1,0:T(8,128)(2,1)} %bitcast.12, f32[6,32,1024]{2,1,0:T(8,128)} %initial.3, ...), custom_call_target="tpu_custom_call" | custom-call | tf_op jit(solution)/shard_map/evolve/pallas_call | solution.py:289
  66.4 12.3 %all_to_all.20 = f32[16,3,4,128]{3,2,1,0:T(4,128)S(1)} all-to-all(f32[16,3,4,128]{3,2,1,0:T(4,128)S(1)} %get-tuple-element.5), channel_id=1, replica_groups=mesh['grp_0'=2,'grp_1'=2,'grp_2'=8,'node_0'=4,'node_1'=2] {'grp_1','node..., dimensions={0} | all-to-all | bytes 196608 | tf_op jit(solution)/shard_map/all_to_all | solution.py:206
  78.8 14.3 %all_to_all.21 = f32[16,3,4,128]{3,2,1,0:T(4,128)S(1)} all-to-all(f32[16,3,4,128]{3,2,1,0:T(4,128)S(1)} %broadcast_in_dim.18), channel_id=1, replica_groups=mesh['grp_0'=2,'grp_1'=2,'grp_2'=8,'node_0'=4,'node_1'=2] {'grp_0','grp_2'}, dimensions={0} | all-to-all | bytes 196608 | tf_op jit(solution)/shard_map/all_to_all | solution.py:202
  93.1 10.3 %all_to_all.22 = f32[16,3,4,128]{3,2,1,0:T(4,128)S(1)} all-to-all(f32[16,3,4,128]{3,2,1,0:T(4,128)S(1)} %broadcast_in_dim.19), channel_id=1, replica_groups=mesh['grp_0'=2,'grp_1'=2,'grp_2'=8,'node_0'=4,'node_1'=2] {'grp_1','node..., dimensions={0} | all-to-all | bytes 196608 | tf_op jit(solution)/shard_map/all_to_all | solution.py:202
  103.4 0.6 copy.14
  (6 shorter events, 0.1 us)
Async XLA Ops:
  4.6 55.3 %all-to-all-start = ((bf16[32,7,32,128]{3,2,1,0:T(8,128)(2,1)}), bf16[32,7,32,128]{3,2,1,0:T(8,128)(2,1)S(1)}, u32[]{:S(2)}, u32[]{:S(2)}) async-start(bf16[32,7,32,128]{3,2,1,0:T(8,128)(2,1)} %pack.1.after), calls=%async_computation | async-start | bytes 3670016 | tf_op jit(solution)/shard_map/all_to_all | solution.py:274
  16.5 1.5 %copy-start = (s32[256,24]{0,1:T(8,128)S(1)}, s32[256,24]{0,1:T(8,128)}, u32[]{:S(2)}) copy-start(s32[256,24]{0,1:T(8,128)} %param.14) | copy-start | bytes 73732
  16.5 1.5 %copy-start.1 = (s32[256]{0:T(256)S(1)}, s32[256]{0:T(256)}, u32[]{:S(2)}) copy-start(s32[256]{0:T(256)} %param.17) | copy-start | bytes 3076

commit v7 on v6

--- a/solution.py
+++ b/solution.py
@@ -59,16 +59,20 @@
     for load in loads:
         load.wait()
 
-    def put(g):
-        return pltpu.make_async_copy(parts.at[g], out.at[g], puts.at[g])
+    together = owners // puts.shape[0]
+
+    def put(i):
+        some = pl.ds(i * together, together)
+        return pltpu.make_async_copy(parts.at[some], out.at[some], puts.at[i])
 
     for g in range(owners):
         code = chosen[0, g * columns + column[0]]
         sub = pl.multiple_of((code & 7) * piece, piece)
         parts[g] = whole[pl.ds(code >> 3, TIMES), :, pl.ds(sub, piece)]
-        put(g).start()
-    for g in range(owners):
-        put(g).wait()
+        if g % together == together - 1:
+            put(g // together).start()
+    for i in range(puts.shape[0]):
+        put(i).wait()
 
 
 def fill_left(own, parcel, left, tiles, piece):
@@ -253,8 +257,8 @@
             pltpu.VMEM((1, counts.shape[0]), jnp.int32),
             pltpu.VMEM((1, counts.shape[0]), jnp.int32),
             pltpu.SMEM((1, counts.shape[0]), jnp.int32),
-            pltpu.SemaphoreType.DMA((4,)),
-            pltpu.SemaphoreType.DMA((owners,)),
+            pltpu.SemaphoreType.DMA((8,)),
+            pltpu.SemaphoreType.DMA((8,)),
             pltpu.SemaphoreType.DMA,
             pltpu.SemaphoreType.DMA((4,)),
             pltpu.SemaphoreType.DMA,

time: 104 us -> 104 us (level)
  no operation moved by 1% of the time
where the time goes in v7:
time: 104 us
  waiting for transfers between devices  41.8 us (40%)
  blocking collectives  36.9 us (35%)
  starting transfers between devices  11.9 us (11%)
  Pallas kernels  11.8 us (11%)
    all_to_all x1, waiting for transfers between devices, body(): lax.all_to_all(packed, GRP, split_axis=0, concat_axis=0, tiled=True)  41.8 us
    all_to_all x2, blocking collectives, to_all(): return lax.all_to_all(copies, axis, split_axis=0, concat_axis=0, tiled=True)  24.6 us
    all_to_all x1, blocking collectives, total_of(): lax.all_to_all(parts, SPREAD, split_axis=0, concat_axis=0, tiled=True)  12.3 us
    all_to_all x1, starting transfers between devices, body(): lax.all_to_all(packed, GRP, split_axis=0, concat_axis=0, tiled=True)  11.9 us
    pallas_call x1, Pallas kernels, body(): pl.pallas_call(functools.partial(evolve_kernel, tiles=tiles, piece=piece,...  6.5 us
    pallas_call x1, Pallas kernels, body(): pl.pallas_call(functools.partial(pack_kernel, columns=columns, piece=piec...  3.91 us
  transfers between devices with their start and end apart: 1, of which 1 were waited for; matrix products, arithmetic and copies ran while one was open for 0% of the time, Pallas kernels for 1%

profile of v7, /device:TPU:1, one launch (start us, length us, event | category | flops | bytes accessed | tf_op | source)
XLA Modules:
  0.0 104.0 jit_solution(1152524684976240149)
XLA Ops:
  0.6 3.9 %pack.1.after = bf16[32,7,32,128]{3,2,1,0:T(8,128)(2,1)} custom-call(s32[1]{0:T(128)} %bitcast.1.group, s32[1]{0:T(128)} %bitcast.2.column, s32[24,256]{1,0:T(8,128)} %bitcast.14, s32[24,256]{1,0:T(8,128)} %bitcast.15, s32[24,256]{1,0:T(8,128)} %bitcast.16, s32[1,256]{1,0:T(1,128)} %bitcast.17, bf16[64,32,1024]{2,1,0:T(8,128)(2,1)} %history.1, ...), custom_call_target="tpu_custom_call" | custom-call | tf_op jit(solution)/shard_map/pack/pallas_call | solution.py:247
  4.6 11.9 %all-to-all-start = ((bf16[32,7,32,128]{3,2,1,0:T(8,128)(2,1)}), bf16[32,7,32,128]{3,2,1,0:T(8,128)(2,1)S(1)}, u32[]{:S(2)}, u32[]{:S(2)}) async-start(bf16[32,7,32,128]{3,2,1,0:T(8,128)(2,1)} %pack.1.after), calls=%async_computation | async-start | bytes 3670016 | tf_op jit(solution)/shard_map/all_to_all | solution.py:278
  16.4 0.0 copy-start
  16.5 0.0 copy-start.1
  16.5 1.4 %hold.1.held = bf16[12,128,512]{2,1,0:T(8,128)(2,1)S(1)} custom-call(bf16[32,7,32,128]{3,2,1,0:T(8,128)(2,1)} %pack.1.after, bf16[24,128,1024]{2,1,0:T(8,128)(2,1)} %bitcast.11), custom_call_target="tpu_custom_call" | custom-call | tf_op jit(solution)/shard_map/hold/pallas_call | solution.py:284
  17.9 0.0 copy-done
  17.9 0.0 copy-done.1
  17.9 0.1 select_reduce_fusion
  18.1 41.8 %all-to-all-done.parcel = bf16[32,7,32,128]{3,2,1,0:T(8,128)(2,1)S(1)} async-done(((bf16[32,7,32,128]{3,2,1,0:T(8,128)(2,1)}), bf16[32,7,32,128]{3,2,1,0:T(8,128)(2,1)S(1)}, u32[]{:S(2)}, u32[]{:S(2)}) %all-to-all-start) | async-done | bytes 1835040 | tf_op jit(solution)/shard_map/all_to_all | solution.py:278
  59.9 6.5 %evolve.1 = (f32[6,32,1024]{2,1,0:T(8,128)}, f32[16,3,4,128]{3,2,1,0:T(4,128)S(1)}) custom-call(s32[24]{0:T(128)S(1)} %broadcast_add_fusion.own, bf16[32,7,32,128]{3,2,1,0:T(8,128)(2,1)S(1)} %all-to-all-done.parcel, bf16[12,128,512]{2,1,0:T(8,128)(2,1)S(1)} %hold.1.held, bf16[24,128,1024]{2,1,0:T(8,128)(2,1)} %bitcast.12, f32[6,32,1024]{2,1,0:T(8,128)} %initial.3, ...), custom_call_target="tpu_custom_call" | custom-call | tf_op jit(solution)/shard_map/evolve/pallas_call | solution.py:293
  66.4 12.3 %all_to_all.20 = f32[16,3,4,128]{3,2,1,0:T(4,128)S(1)} all-to-all(f32[16,3,4,128]{3,2,1,0:T(4,128)S(1)} %get-tuple-element.5), channel_id=1, replica_groups=mesh['grp_0'=2,'grp_1'=2,'grp_2'=8,'node_0'=4,'node_1'=2] {'grp_1','node..., dimensions={0} | all-to-all | bytes 196608 | tf_op jit(solution)/shard_map/all_to_all | solution.py:210
  78.8 14.3 %all_to_all.21 = f32[16,3,4,128]{3,2,1,0:T(4,128)S(1)} all-to-all(f32[16,3,4,128]{3,2,1,0:T(4,128)S(1)} %broadcast_in_dim.18), channel_id=1, replica_groups=mesh['grp_0'=2,'grp_1'=2,'grp_2'=8,'node_0'=4,'node_1'=2] {'grp_0','grp_2'}, dimensions={0} | all-to-all | bytes 196608 | tf_op jit(solution)/shard_map/all_to_all | solution.py:206
  93.1 10.3 %all_to_all.22 = f32[16,3,4,128]{3,2,1,0:T(4,128)S(1)} all-to-all(f32[16,3,4,128]{3,2,1,0:T(4,128)S(1)} %broadcast_in_dim.19), channel_id=1, replica_groups=mesh['grp_0'=2,'grp_1'=2,'grp_2'=8,'node_0'=4,'node_1'=2] {'grp_1','node..., dimensions={0} | all-to-all | bytes 196608 | tf_op jit(solution)/shard_map/all_to_all | solution.py:206
  103.4 0.6 copy.14
  (6 shorter events, 0.1 us)
Async XLA Ops:
  4.6 55.3 %all-to-all-start = ((bf16[32,7,32,128]{3,2,1,0:T(8,128)(2,1)}), bf16[32,7,32,128]{3,2,1,0:T(8,128)(2,1)S(1)}, u32[]{:S(2)}, u32[]{:S(2)}) async-start(bf16[32,7,32,128]{3,2,1,0:T(8,128)(2,1)} %pack.1.after), calls=%async_computation | async-start | bytes 3670016 | tf_op jit(solution)/shard_map/all_to_all | solution.py:278
  16.4 1.5 %copy-start = (s32[256,24]{0,1:T(8,128)S(1)}, s32[256,24]{0,1:T(8,128)}, u32[]{:S(2)}) copy-start(s32[256,24]{0,1:T(8,128)} %param.14) | copy-start | bytes 73732
  16.5 1.5 %copy-start.1 = (s32[256]{0:T(256)S(1)}, s32[256]{0:T(256)}, u32[]{:S(2)}) copy-start(s32[256]{0:T(256)} %param.17) | copy-start | bytes 3076
